TPU v7x, 32 devices: a whole 2x2x4 slice. The times are simulated.
32 devices in a mesh: row: 4 (over y, x), col: 8 (over z, core).
Axes of the slice: x: 2, y: 2, z: 4, core: 2. Of those that a mesh axis runs over, the one named last changes fastest.
Arguments:
- view_one: bfloat16 [2048, 8192], P('row', 'col'), may hold values from -6 to 6
- view_two: bfloat16 [2048, 8192], P('row', 'col'), may hold values from -6 to 6
- pair_weights: bfloat16 [8192, 8192], P('row', 'col'), may hold values from 0.25 to 2.5
Outputs:
- first_grad: bfloat16 [2048, 8192], P('row', 'col')
- second_grad: bfloat16 [2048, 8192], P('row', 'col')
All inputs are finite; a program needn't handle non-finite values.
Results may differ from a plain program's by a relative error of at most 0.004.
Values may be sent and summed in bfloat16 or wider, within the bound.
A program may use at most 128 MiB of HBM per device.

v0:
```python
import jax
import jax.numpy as jnp
from jax import lax
from jax.experimental import pallas as pl
from jax.experimental.pallas import tpu as pltpu
from jax.sharding import PartitionSpec as P

MESH = pl.DeviceIdType.MESH
CORES = 2
PIECES = 4


def arrived(ref, sem):
    pltpu.make_async_copy(ref, ref, sem).wait()


def remote(src, dst, send, recv, device):
    return pltpu.make_async_remote_copy(
        src_ref=src, dst_ref=dst, send_sem=send, recv_sem=recv, device_id=device, device_id_type=MESH
    )


def gather_kernel(rows, one_ref, two_ref, one_out, two_out, one_held, held, load_sem, one_send, one_recv, pair_send,
                  pair_recv, up_send, down_send, held_recv, swap_send, swap_recv, twin_send, twin_recv):
    samples, width = two_ref.shape
    piece = samples // PIECES
    row, col = lax.axis_index("row"), lax.axis_index("col")
    z, core = lax.div(col, CORES), lax.rem(col, CORES)
    twin = (row, col + 1 - 2 * core)
    core_cols = pl.ds(pl.multiple_of(core * width, width), width)
    twin_cols = pl.ds(pl.multiple_of((1 - core) * width, width), width)

    def block_rows(index):
        return pl.ds(pl.multiple_of(index * samples, samples), samples)

    def piece_rows(index, q):
        return pl.ds(pl.multiple_of(index * samples + q * piece, piece), piece)

    def held_piece(index, q):
        return held.at[index, pl.ds(q * piece, piece)]

    def up(index, q):
        part = held_piece(index, q)
        return remote(part, part, up_send.at[index, q], held_recv.at[index, q], (row, col + CORES))

    def down(index, q):
        part = held_piece(index, q)
        return remote(part, part, down_send.at[index, q], held_recv.at[index, q], (row, col - CORES))

    def swap(index, q):
        return remote(held_piece(index, q), two_out.at[piece_rows(row, q), core_cols], swap_send.at[index, q],
                      swap_recv.at[row, q], (index, col))

    def route(index, q):
        @pl.when(index != row)
        def _():
            swap(index, q).start()

        @pl.when(index == row)
        def _():
            pltpu.make_async_copy(held_piece(index, q), two_out.at[piece_rows(row, q), core_cols],
                                  swap_recv.at[row, q]).start()

    def one_copy(step):
        target = lax.rem(row + step, rows)
        return remote(one_held, one_out.at[block_rows(row), pl.ds(0, width)], one_send.at[step], one_recv.at[row],
                      (target, col))

    def one_twin(index):
        part = one_out.at[block_rows(index), pl.ds(0, width)]
        return remote(part, one_out.at[block_rows(index), pl.ds(width, width)], pair_send.at[index],
                      pair_recv.at[index], twin)

    def two_twin(index, q):
        part = two_out.at[piece_rows(index, q), core_cols]
        return remote(part, part, twin_send.at[index, q], twin_recv.at[index, q], twin)

    def pass_up(index, q):
        @pl.when(z < rows - 1)
        def _():
            up(index, q).start()

    def pass_down(index, q):
        @pl.when(z > 0)
        def _():
            down(index, q).start()

    def own(q):
        pass_up(z, q)
        pass_down(z, q)
        route(z, q)

    load_two = pltpu.make_async_copy(two_ref, held.at[z], load_sem.at[0])
    load_one = pltpu.make_async_copy(one_ref, one_held, load_sem.at[1])
    load_two.start()
    load_one.start()
    load_two.wait()
    own(0)
    load_one.wait()
    for step in range(1, rows):
        one_copy(step).start()
    pltpu.make_async_copy(one_held, one_out.at[block_rows(row), pl.ds(0, width)], one_recv.at[row]).start()

    for q in range(PIECES):
        if q + 1 < PIECES:
            own(q + 1)
        for step in range(1, rows):
            @pl.when(z >= step)
            def _(step=step, q=q):
                arrived(held_piece(z - step, q), held_recv.at[z - step, q])
                pass_up(z - step, q)
                route(z - step, q)

            @pl.when(z + step < rows)
            def _(step=step, q=q):
                arrived(held_piece(z + step, q), held_recv.at[z + step, q])
                pass_down(z + step, q)
                route(z + step, q)

    for step in range(rows):
        index = lax.rem(row - step + rows, rows)
        arrived(one_out.at[block_rows(index), pl.ds(0, width)], one_recv.at[index])
        one_twin(index).start()
    for q in range(PIECES):
        for step in range(rows):
            index = lax.rem(row - step + rows, rows)
            arrived(two_out.at[piece_rows(index, q), core_cols], swap_recv.at[index, q])
            two_twin(index, q).start()

    for index in range(rows):
        one_twin(index).wait_send()
        arrived(one_out.at[block_rows(index), pl.ds(width, width)], pair_recv.at[index])
        for q in range(PIECES):
            two_twin(index, q).wait_send()
            arrived(two_out.at[piece_rows(index, q), twin_cols], twin_recv.at[index, q])

            @pl.when(index != row)
            def _(index=index, q=q):
                swap(index, q).wait_send()

            @pl.when(jnp.logical_and(z < rows - 1, index <= z))
            def _(index=index, q=q):
                up(index, q).wait_send()

            @pl.when(jnp.logical_and(z > 0, index >= z))
            def _(index=index, q=q):
                down(index, q).wait_send()
    for step in range(1, rows):
        one_copy(step).wait_send()


def scatter_kernel(rows, one_ref, two_ref, weighted_ref, first_out, second_out, one_held, two_held, weighted, theirs,
                   first_sent, parts, second_sent, moved, from_below, from_above, load_sem, twin_sem, first_send,
                   first_recv, move_send, move_recv, up_send, up_recv, down_send, down_recv):
    samples, width = first_out.shape
    tile = width // PIECES
    row, col = lax.axis_index("row"), lax.axis_index("col")
    z, core = lax.div(col, CORES), lax.rem(col, CORES)

    def half(which):
        return pl.ds(pl.multiple_of(which * width, width), width)

    def move(target, q):
        return remote(second_sent.at[q, target], moved.at[q, row], move_send.at[q, target], move_recv.at[q, row],
                      (target, col))

    def first_copy(target, q):
        return remote(first_sent.at[q, target], parts.at[q, row], first_send.at[q, target], first_recv.at[q, row],
                      (target, col))

    def up(index, q):
        return remote(moved.at[q, index], from_below.at[q, index], up_send.at[q, index], up_recv.at[q, index],
                      (row, col + CORES))

    def down(index, q):
        return remote(moved.at[q, index], from_above.at[q, index], down_send.at[q, index], down_recv.at[q, index],
                      (row, col - CORES))

    def first_tile(target, q):
        cols = pl.ds(pl.multiple_of(q * tile, tile), tile)
        mine = two_held[pl.ds(pl.multiple_of(target * samples, samples), samples), :]
        return jnp.dot(mine, weighted[:, cols], preferred_element_type=jnp.float32).astype(jnp.bfloat16)

    def second_tile(target, q):
        here = pl.ds(pl.multiple_of(target * samples, samples), samples)
        contract = (((1,), (1,)), ((), ()))
        near = weighted[pl.ds(pl.multiple_of(core * width + q * tile, tile), tile), :]
        far = theirs[pl.ds(pl.multiple_of(q * tile, tile), tile), :]
        total = lax.dot_general(one_held[here, pl.ds(0, width)], near, contract, preferred_element_type=jnp.float32)
        total += lax.dot_general(one_held[here, pl.ds(width, width)], far, contract,
                                 preferred_element_type=jnp.float32)
        return total.astype(jnp.bfloat16)

    exchange = remote(weighted_ref.at[half(1 - core)], theirs, twin_sem.at[0], twin_sem.at[1],
                      (row, col + 1 - 2 * core))
    exchange.start()
    loads = [pltpu.make_async_copy(src, dst, load_sem.at[i]) for i, (src, dst) in enumerate(
        ((weighted_ref, weighted), (two_ref, two_held), (one_ref, one_held)))]
    for load in loads:
        load.start()
    loads[0].wait()
    loads[1].wait()

    def own_first(q, _):
        parts[q, row] = first_tile(row, q)
        return 0

    lax.fori_loop(0, PIECES, own_first, 0)
    loads[2].wait()
    exchange.wait()

    def seconds(i, _):
        q, step = lax.div(i, rows), lax.rem(i, rows) + 1
        target = lax.rem(row + step, rows)
        value = second_tile(target, q)

        @pl.when(target == row)
        def _():
            moved[q, row] = value

        @pl.when(target != row)
        def _():
            second_sent[q, target] = value
            move(target, q).start()

        return 0

    lax.fori_loop(0, PIECES * rows, seconds, 0)

    def firsts(i, _):
        q, step = lax.div(i, rows - 1), lax.rem(i, rows - 1) + 1
        target = lax.rem(row + step, rows)
        first_sent[q, target] = first_tile(target, q)
        first_copy(target, q).start()
        return 0

    lax.fori_loop(0, PIECES * (rows - 1), firsts, 0)

    def settle(index, q):
        @pl.when(index != row)
        def _():
            arrived(moved.at[q, index], move_recv.at[q, index])

    def chain(i, _):
        q, turn = lax.div(i, rows - 1), lax.rem(i, rows - 1)
        above = rows - 1 - (turn - z)
        below = turn - (rows - 1 - z)

        @pl.when(jnp.logical_and(turn >= z, above > z))
        def _():
            settle(above, q)

            @pl.when(z > 0)
            def _():
                arrived(from_below.at[q, above], up_recv.at[q, above])
                moved[q, above] = (moved[q, above].astype(jnp.float32)
                                   + from_below[q, above].astype(jnp.float32)).astype(jnp.bfloat16)

            up(above, q).start()

        @pl.when(jnp.logical_and(below >= 0, below < z))
        def _():
            settle(below, q)

            @pl.when(z < rows - 1)
            def _():
                arrived(from_above.at[q, below], down_recv.at[q, below])
                moved[q, below] = (moved[q, below].astype(jnp.float32)
                                   + from_above[q, below].astype(jnp.float32)).astype(jnp.bfloat16)

            down(below, q).start()

        return 0

    lax.fori_loop(0, PIECES * (rows - 1), chain, 0)

    for q in range(PIECES):
        cols = pl.ds(q * tile, tile)
        for step in range(1, rows):
            index = lax.rem(row + step, rows)
            arrived(parts.at[q, index], first_recv.at[q, index])
        total = parts[q, 0].astype(jnp.float32)
        for index in range(1, rows):
            total += parts[q, index].astype(jnp.float32)
        first_out[:, cols] = total.astype(first_out.dtype)
    for q in range(PIECES):
        cols = pl.ds(q * tile, tile)
        settle(z, q)

        @pl.when(z > 0)
        def _(q=q):
            arrived(from_below.at[q, z], up_recv.at[q, z])

        @pl.when(z < rows - 1)
        def _(q=q):
            arrived(from_above.at[q, z], down_recv.at[q, z])

        @pl.when(z == 0)
        def _(q=q, cols=cols):
            second_out[:, cols] = (moved[q, z].astype(jnp.float32)
                                   + from_above[q, z].astype(jnp.float32)).astype(second_out.dtype)

        @pl.when(z == rows - 1)
        def _(q=q, cols=cols):
            second_out[:, cols] = (moved[q, z].astype(jnp.float32)
                                   + from_below[q, z].astype(jnp.float32)).astype(second_out.dtype)

        @pl.when(jnp.logical_and(z > 0, z < rows - 1))
        def _(q=q, cols=cols):
            second_out[:, cols] = (moved[q, z].astype(jnp.float32) + from_below[q, z].astype(jnp.float32)
                                   + from_above[q, z].astype(jnp.float32)).astype(second_out.dtype)

    for q in range(PIECES):
        for step in range(1, rows):
            target = lax.rem(row + step, rows)
            move(target, q).wait_send()
            first_copy(target, q).wait_send()
        for index in range(rows):
            @pl.when(index > z)
            def _(index=index, q=q):
                up(index, q).wait_send()

            @pl.when(index < z)
            def _(index=index, q=q):
                down(index, q).wait_send()


def gather(rows, view_one, view_two):
    samples, width = view_one.shape
    whole = jax.ShapeDtypeStruct((rows * samples, CORES * width), jnp.bfloat16)
    any_space = pl.BlockSpec(memory_space=pl.ANY)
    dma = pltpu.SemaphoreType.DMA
    return pl.pallas_call(
        lambda *refs: gather_kernel(rows, *refs),
        out_shape=(whole, whole),
        in_specs=[any_space] * 2,
        out_specs=(any_space, any_space),
        scratch_shapes=[
            pltpu.VMEM((samples, width), jnp.bfloat16),
            pltpu.VMEM((rows, samples, width), jnp.bfloat16),
            dma((2,)),
        ] + [dma((rows,))] * 4 + [dma((rows, PIECES))] * 7,
        compiler_params=pltpu.CompilerParams(has_side_effects=True),
        name="gather_views",
    )(view_one, view_two)


def scatter(rows, one_pair, two_rows, weighted):
    height, width = weighted.shape
    samples = one_pair.shape[0] // rows
    own = jax.ShapeDtypeStruct((samples, width), jnp.bfloat16)
    any_space = pl.BlockSpec(memory_space=pl.ANY)
    vmem = pl.BlockSpec(memory_space=pltpu.VMEM)
    blocks = pltpu.VMEM((PIECES, rows, samples, width // PIECES), jnp.bfloat16)
    views = pltpu.VMEM(one_pair.shape, jnp.bfloat16)
    dma = pltpu.SemaphoreType.DMA
    return pl.pallas_call(
        lambda *refs: scatter_kernel(rows, *refs),
        out_shape=(own, own),
        in_specs=[any_space] * 3,
        out_specs=(vmem, vmem),
        scratch_shapes=[
            views,
            views,
            pltpu.VMEM((height, width), jnp.bfloat16),
            pltpu.VMEM((width, width), jnp.bfloat16),
        ] + [blocks] * 6 + [dma((3,)), dma((2,))] + [dma((PIECES, rows))] * 8,
        compiler_params=pltpu.CompilerParams(has_side_effects=True, vmem_limit_bytes=60 * 2**20),
        name="scatter_grads",
    )(one_pair, two_rows, weighted)


def per_device(view_one, view_two, pair_weights):
    rows = lax.axis_size("row")
    samples = view_one.shape[0] * rows
    local_rows, local_cols = pair_weights.shape
    row, col = lax.axis_index("row"), lax.axis_index("col")
    one_pair, two_rows = gather(rows, view_one, view_two)
    summed = lax.dot_general(
        two_rows, one_pair[:, :local_cols], (((0,), (0,)), ((), ())), preferred_element_type=jnp.float32
    )
    row_ids = row * local_rows + lax.broadcasted_iota(jnp.int32, (local_rows, local_cols), 0)
    col_ids = col * local_cols + lax.broadcasted_iota(jnp.int32, (local_rows, local_cols), 1)
    identity = jnp.where(row_ids == col_ids, 1.0, 0.0).astype(jnp.float32)
    weighted = (pair_weights.astype(jnp.float32) * (summed / samples - identity)).astype(jnp.bfloat16)
    return scatter(rows, one_pair, two_rows, weighted)


def solution(mesh):
    placed = (P("row", "col"), P("row", "col"), P("row", "col"))
    return jax.shard_map(
        per_device,
        mesh=mesh,
        in_specs=placed,
        out_specs=(P("row", "col"), P("row", "col")),
        check_vma=False,
    )
```

profile of v0, /device:TPU:0, one launch (start us, length us, event | category | flops | bytes accessed | tf_op | source)
XLA Modules:
  0.0 236.0 jit_solution(10162655978969572213)
XLA Ops:
  0.7 104.3 %gather_views.1 = (bf16[2048,2048]{1,0:T(8,128)(2,1)}, bf16[2048,2048]{1,0:T(8,128)(2,1)}) custom-call(bf16[512,1024]{1,0:T(8,128)(2,1)} %refs_0_.1, bf16[512,1024]{1,0:T(8,128)(2,1)} %refs_1_.1), custom_call_target="tpu_custom_call" | custom-call | tf_op jit(solution)/shard_map/gather_views/pallas_call | solution.py:333
  104.9 16.4 %multiply_convert_fusion.refs_2_ = bf16[2048,1024]{1,0:T(8,128)(2,1)} fusion(bf16[2048,1024]{1,0:T(8,128)(2,1)} %param.5, bf16[2048,2048]{1,0:T(8,128)(2,1)} %get-tuple-element.5.refs_1_, s32[1024]{0:T(1024)S(1)} %iota_add_fusion.1, bf16[2048,2048]{1,0:T(8,128)(2,1)} %get-tuple-element.4.refs_0_, s32[2048]{0:T(1024)S(1)} %iota_add_fusion), kind=kOutput, calls=%fused_computation | convolution fusion | flops 8604614656 | bytes 20983808 | tf_op jit(solution)/shard_map/dot_general | solution.py:379
  121.3 110.2 %scatter_grads.1 = (bf16[512,1024]{1,0:T(8,128)(2,1)}, bf16[512,1024]{1,0:T(8,128)(2,1)}) custom-call(bf16[2048,2048]{1,0:T(8,128)(2,1)} %get-tuple-element.4.refs_0_, bf16[2048,2048]{1,0:T(8,128)(2,1)} %get-tuple-element.5.refs_1_, bf16[2048,1024]{1,0:T(8,128)(2,1)} %multiply_convert_fusion.refs_2_), custom_call_target="tpu_custom_call" | custom-call | tf_op jit(solution)/shard_map/scatter_grads/pallas_call | solution.py:357
  231.5 2.3 copy.7
  233.8 2.3 copy.8
  (2 shorter events, 0.0 us)
where the time goes:
time: 236 us
  Pallas kernels  214 us (91%)
  matrix products  16.4 us (7%)
  local copies, waits for them, and re-layouts  4.52 us (2%)
    pallas_call x1, Pallas kernels, scatter(): pl.pallas_call(lambda *refs: scatter_kernel(rows, *refs), out_shape=(own,...  110 us
    pallas_call x1, Pallas kernels, gather(): pl.pallas_call(lambda *refs: gather_kernel(rows, *refs), out_shape=(whole...  104 us
    dot_general x1, matrix products, per_device(): lax.dot_general(two_rows, one_pair[:, :local_cols], (((0,), (0,)), ((), (...  16.4 us

commit v1 on v0

v1 whole, which is shorter than its diff:
```python
import jax
import jax.numpy as jnp
from jax import lax
from jax.experimental import pallas as pl
from jax.experimental.pallas import tpu as pltpu
from jax.sharding import PartitionSpec as P

MESH = pl.DeviceIdType.MESH
CORES = 2
HALVES = 2
PAIR = 2


def arrived(ref, sem):
    pltpu.make_async_copy(ref, ref, sem).wait()


def remote(src, dst, send, recv, device):
    return pltpu.make_async_remote_copy(
        src_ref=src, dst_ref=dst, send_sem=send, recv_sem=recv, device_id=device, device_id_type=MESH
    )


def at(start, size):
    return pl.ds(pl.multiple_of(start, size), size)


def pick(index, values):
    chosen = jnp.int32(values[0])
    for i, value in enumerate(values[1:], 1):
        chosen = jnp.where(index == i, value, chosen)
    return chosen


def step_kernel(rows, strip, one_ref, two_ref, pair_ref, first_out, second_out, two_held, two_own, two_twin, turned, one,
                pair, weighted, theirs, below, above, second_sent, second_sum, first_sent, first_wide, first_deep,
                wide_sum, deep_sum, load_sem, two_recv, feed_send, up_send, down_send, two_pair, one_send, one_recv,
                one_pair, weight_sem, theirs_sem, chain_send, below_recv, above_recv, spread_send, spread_recv,
                first_send, wide_recv, deep_recv, wide_last, deep_last):
    samples, width = two_ref.shape
    wide = PAIR
    deep = rows // wide
    strips = width // strip
    part = samples // HALVES
    chunk = rows * HALVES
    pieces = strips * chunk
    tile = min(width, 512)
    tiles = width // tile
    parts = CORES * tiles
    row, col = lax.axis_index("row"), lax.axis_index("col")
    z, core = lax.div(col, CORES), lax.rem(col, CORES)
    other = 1 - core
    a, b = lax.rem(row, wide), lax.div(row, wide)
    home = z == row
    reach = jnp.where(z > row, rows - 1 - row, jnp.where(z < row, row, jnp.maximum(row, rows - 1 - row)))
    back = reach - jnp.abs(z - row)
    last = back == 0
    twin = (row, col + 1 - 2 * core)

    def device(target, level):
        return (target, level * CORES + core)

    def half(h):
        return at(h * part, part)

    def cols(q):
        return at(q * strip, strip)

    def split(t):
        return lax.div(t, chunk), lax.rem(lax.div(t, HALVES), rows), lax.rem(t, HALVES)

    def two_piece(t):
        q, i, h = split(t)
        return two_own.at[lax.rem(row + i, rows), half(h), cols(q)]

    def two_up(t):
        return remote(two_piece(t), two_piece(t), up_send.at[t], two_recv.at[t], device(row, z + 1))

    def two_down(t):
        return remote(two_piece(t), two_piece(t), down_send.at[t], two_recv.at[t], device(row, z - 1))

    def feed(q, h):
        t = q * chunk + lax.rem(row - z + rows, rows) * HALVES + h
        return remote(two_held.at[half(h), cols(q)], two_own.at[row, half(h), cols(q)], feed_send.at[q, h],
                      two_recv.at[t], device(z, z))

    def own_two(q, h):
        return pltpu.make_async_copy(two_ref.at[half(h), cols(q)], two_own.at[row, half(h), cols(q)],
                                     two_recv.at[q * chunk + h])

    def feeds(q):
        @pl.when(z != row)
        def _():
            for h in range(HALVES):
                feed(q, h).start()

    def two_swap(q):
        return remote(two_own.at[:, :, cols(q)], two_twin.at[:, :, cols(q)], two_pair.at[0, q], two_pair.at[1, q], twin)

    def one_block(block, h):
        return one.at[core, block, half(h)]

    def one_copy(block, h, target):
        return remote(one_block(block, h), one_block(block, h), one_send.at[block, h, target], one_recv.at[block, h],
                      (target, col))

    def one_swap(block, h):
        return remote(one_block(block, h), one_block(block, h), one_pair.at[0, block, h], one_pair.at[1, block, h],
                      twin)

    def block_of(over, down):
        return lax.rem(b + down, deep) * wide + lax.rem(a + over, wide)

    across = [(over, 0) for over in range(1, wide)]
    along = [(0, down) for down in range(1, deep)]
    far = [(over, down) for over in range(1, wide) for down in range(1, deep)]

    def take_one(block, h):
        arrived(one_block(block, h), one_recv.at[block, h])
        one_swap(block, h).start()

    def weights_swap():
        return remote(pair_ref.at[at(other * width, width)], pair.at[core], weight_sem.at[0], weight_sem.at[1], twin)

    def theirs_swap(q):
        return remote(weighted.at[other, cols(q)], theirs.at[cols(q)], theirs_sem.at[0, q], theirs_sem.at[1, q], twin)

    load_two = pltpu.make_async_copy(two_ref, two_held, load_sem.at[0])
    load_one = pltpu.make_async_copy(one_ref, one.at[core, row], load_sem.at[1])
    load_pair = pltpu.make_async_copy(pair_ref.at[at(core * width, width)], pair.at[core], load_sem.at[2])

    load_two.start()

    @pl.when(home)
    def _():
        for q in range(strips):
            for h in range(HALVES):
                own_two(q, h).start()

    load_one.start()
    load_pair.start()
    load_two.wait()
    feeds(0)
    load_one.wait()
    for h in range(HALVES):
        for over, down in across:
            one_copy(row, h, block_of(over, down)).start()
        for over, down in along:
            one_copy(row, HALVES - 1 - h, block_of(over, down)).start()
    for h in range(HALVES):
        one_swap(row, h).start()
    weights_swap().start()
    if strips > 1:
        feeds(1)

    def relay_one():
        for over, down in across:
            block = block_of(over, down)
            take_one(block, 0)
            for _, other_down in along:
                one_copy(block, 0, block_of(0, other_down)).start()
        for over, down in along:
            block = block_of(over, down)
            take_one(block, 1)
            for other_over, _ in across:
                one_copy(block, 1, block_of(other_over, 0)).start()
        for q in range(2, strips):
            feeds(q)

    def finish_one():
        for over, down in across:
            take_one(block_of(over, down), 1)
        for over, down in along:
            take_one(block_of(over, down), 0)
        for over, down in far:
            take_one(block_of(over, down), 0)
            take_one(block_of(over, down), 1)
        for block in range(rows):
            for h in range(HALVES):
                arrived(one.at[other, block, half(h)], one_pair.at[1, block, h])
        load_pair.wait()
        arrived(pair.at[other], weight_sem.at[1])

    def correlate(q, p):
        side, i = lax.div(p, tiles), lax.rem(p, tiles)

        @pl.when(p == 0)
        def _():
            turned[...] = two_own[:, :, cols(q)].reshape(rows * samples, strip).T

        columns = at(i * tile, tile)
        total = jnp.dot(turned[...], one[side, :, :, columns].reshape(rows * samples, tile),
                        preferred_element_type=jnp.float32)
        row_ids = (row * CORES + core) * width + q * strip + lax.broadcasted_iota(jnp.int32, total.shape, 0)
        col_ids = (z * CORES + side) * width + i * tile + lax.broadcasted_iota(jnp.int32, total.shape, 1)
        identity = jnp.where(row_ids == col_ids, 1.0, 0.0).astype(jnp.float32)
        scale = pair[side, cols(q), columns].astype(jnp.float32)
        weighted[side, cols(q), columns] = (scale * (total / (rows * samples) - identity)).astype(jnp.bfloat16)

        @pl.when(p == parts - 1)
        def _():
            theirs_swap(q).start()

    def chain_up(g):
        return remote(second_sent.at[g], below.at[g], chain_send.at[g], below_recv.at[g], device(row, z + 1))

    def chain_down(g):
        return remote(second_sent.at[g], above.at[g], chain_send.at[g], above_recv.at[g], device(row, z - 1))

    def spread(g):
        q, i, h = split(g)
        return remote(second_sent.at[g], second_out.at[half(h), cols(q)], spread_send.at[g], spread_recv.at[q, h],
                      device(lax.rem(row + 1 + i, rows), z))

    from_below = jnp.logical_and(z > 0, z <= row)
    from_above = jnp.logical_and(z < rows - 1, z >= row)

    def second_piece(g):
        q, i, h = split(g)
        target = lax.rem(row + 1 + i, rows)
        contract = (((1,), (1,)), ((), ()))
        second_sum[...] = (
            lax.dot_general(one[0, target, half(h)], weighted[0, cols(q)], contract, preferred_element_type=jnp.float32)
            + lax.dot_general(one[1, target, half(h)], weighted[1, cols(q)], contract,
                              preferred_element_type=jnp.float32))

        @pl.when(from_below)
        def _():
            arrived(below.at[g], below_recv.at[g])
            second_sum[...] += below[g].astype(jnp.float32)

        @pl.when(from_above)
        def _():
            arrived(above.at[g], above_recv.at[g])
            second_sum[...] += above[g].astype(jnp.float32)

        keep = jnp.logical_and(home, i == rows - 1)

        @pl.when(keep)
        def _():
            second_out[half(h), cols(q)] = second_sum[...].astype(jnp.bfloat16)

        @pl.when(jnp.logical_not(keep))
        def _():
            second_sent[g] = second_sum[...].astype(jnp.bfloat16)

        @pl.when(z < row)
        def _():
            chain_up(g).start()

        @pl.when(z > row)
        def _():
            chain_down(g).start()

        @pl.when(jnp.logical_and(home, i != rows - 1))
        def _():
            spread(g).start()

    lead = [(0, over, down) for over, _ in across for down in range(deep)]
    lead_deep = [(1, over, down) for _, down in along for over in range(wide)]
    order = []
    for i in range(max(len(lead), len(lead_deep))):
        order += lead[::-1][i:i + 1] + lead_deep[::-1][i:i + 1]
    opening = len(order)
    order += [(0, 0, down) for _, down in along] + [(1, over, 0) for over, _ in across] + [(0, 0, 0), (1, 0, 0)]

    def unit(u):
        h = pick(u, [entry[0] for entry in order])
        over = pick(u, [entry[1] for entry in order])
        down = pick(u, [entry[2] for entry in order])
        return h, over, down, block_of(over, down)

    def first_hop(u):
        h, over, down, target = unit(u)
        flat = jnp.where(h == 0, (over - 1) * deep + lax.div(target, wide), (down - 1) * wide + lax.rem(target, wide))
        return h, over, down, target, flat

    def wide_open(u):
        h, over, down, target, flat = first_hop(u)
        return remote(first_sent.at[target, half(h)], first_wide.at[flat], first_send.at[u], wide_recv.at[flat],
                      (b * wide + lax.rem(a + over, wide), col))

    def deep_open(u):
        h, over, down, target, flat = first_hop(u)
        return remote(first_sent.at[target, half(h)], first_deep.at[flat], first_send.at[u], deep_recv.at[flat],
                      (lax.rem(b + down, deep) * wide + a, col))

    def deep_close(u):
        h, over, down, target = unit(u)
        return remote(first_sent.at[target, half(h)], deep_sum.at[down - 1], first_send.at[u], deep_last.at[down - 1],
                      (target, col))

    def wide_close(u):
        h, over, down, target = unit(u)
        return remote(first_sent.at[target, half(h)], wide_sum.at[over - 1], first_send.at[u], wide_last.at[over - 1],
                      (target, col))

    def first_tile(target, h, columns):
        return (jnp.dot(two_own[target, half(h)], weighted[core, :, columns], preferred_element_type=jnp.float32)
                + jnp.dot(two_twin[target, half(h)], theirs[:, columns], preferred_element_type=jnp.float32))

    def first_opening(u):
        h, over, down, target = unit(u)

        def body(i, _):
            columns = at(i * tile, tile)
            first_sent[target, half(h), columns] = first_tile(target, h, columns).astype(jnp.bfloat16)
            return 0

        lax.fori_loop(0, tiles, body, 0)

        @pl.when(h == 0)
        def _():
            wide_open(u).start()

        @pl.when(h == 1)
        def _():
            deep_open(u).start()

    def first_closing(u):
        h, over, down, target = unit(u)

        @pl.when(h == 0)
        def _():
            for over_ in range(1, wide):
                flat = (over_ - 1) * deep + lax.div(target, wide)
                arrived(first_wide.at[flat], wide_recv.at[flat])

        @pl.when(h == 1)
        def _():
            for down_ in range(1, deep):
                flat = (down_ - 1) * wide + lax.rem(target, wide)
                arrived(first_deep.at[flat], deep_recv.at[flat])

        def body(i, _):
            columns = at(i * tile, tile)
            total = first_tile(target, h, columns)

            @pl.when(h == 0)
            def _():
                acc = total
                for over_ in range(1, wide):
                    acc += first_wide[(over_ - 1) * deep + lax.div(target, wide), :, columns].astype(jnp.float32)
                first_sent[target, half(h), columns] = acc.astype(jnp.bfloat16)

            @pl.when(h == 1)
            def _():
                acc = total
                for down_ in range(1, deep):
                    acc += first_deep[(down_ - 1) * wide + lax.rem(target, wide), :, columns].astype(jnp.float32)
                first_sent[target, half(h), columns] = acc.astype(jnp.bfloat16)

            return 0

        lax.fori_loop(0, tiles, body, 0)

        @pl.when(h == 0)
        def _():
            deep_close(u).start()

        @pl.when(h == 1)
        def _():
            wide_close(u).start()

    closing = len(order) - 2 - opening
    lag = jnp.where(last, 0, jnp.minimum(6, 4 * back - 2))
    second_lag = chunk - 1 + jnp.where(last, 0, 2 + 4 * back)
    done = jnp.where(last, pieces, pieces - 1 + lag + parts)
    open_slot = done + 1
    close_slot = jnp.maximum(open_slot + 2, pieces + 8 + 2 * back)
    relay_slot = jnp.maximum(0, 4 - 2 * jnp.abs(z - row))
    slots = pieces + chunk + 2 + 4 * rows
    each = (opening + 1) // 2

    def slot(t, _):
        @pl.when(t == relay_slot)
        def _():
            relay_one()

        @pl.when(t < pieces)
        def _():
            arrived(two_piece(t), two_recv.at[t])

            @pl.when(jnp.logical_and(z >= row, z < rows - 1))
            def _():
                two_up(t).start()

            @pl.when(jnp.logical_and(z <= row, z > 0))
            def _():
                two_down(t).start()

            @pl.when(lax.rem(t, chunk) == chunk - 1)
            def _():
                two_swap(lax.div(t, chunk)).start()

        since = t - (chunk - 1) - lag

        @pl.when(since == 0)
        def _():
            finish_one()

        q, p = lax.div(since, chunk), lax.rem(since, chunk)
        live = jnp.logical_and(since >= 0, q < strips)
        low = jnp.where(jnp.logical_or(last, jnp.logical_not(live)), 0, p)
        high = jnp.where(last, jnp.where(p == 0, parts, 0), jnp.where(p < parts, p + 1, 0))
        high = jnp.where(live, high, 0)

        def piece(i, _):
            correlate(q, i)
            return 0

        lax.fori_loop(low, high, piece, 0)

        @pl.when(t == open_slot)
        def _():
            for q_ in range(strips):
                arrived(two_twin.at[:, :, cols(q_)], two_pair.at[1, q_])
                arrived(theirs.at[cols(q_)], theirs_sem.at[1, q_])

        g = t - second_lag

        @pl.when(jnp.logical_and(g >= 0, g < pieces))
        def _():
            second_piece(g)

        first = jnp.where(t == open_slot, 0, jnp.where(t == open_slot + 1, each, opening))
        final = jnp.where(t == open_slot, each, opening)

        def opener(u, _):
            first_opening(u)
            return 0

        lax.fori_loop(first, final, opener, 0)

        def closer(u, _):
            first_closing(u)
            return 0

        lax.fori_loop(opening, jnp.where(t == close_slot, opening + closing, opening), closer, 0)
        return 0

    lax.fori_loop(0, slots, slot, 0)

    for _, down in along:
        arrived(deep_sum.at[down - 1], deep_last.at[down - 1])
    for over, _ in across:
        arrived(wide_sum.at[over - 1], wide_last.at[over - 1])
        for d in range(deep):
            @pl.when(d == b)
            def _(over=over, d=d):
                flat = (over - 1) * deep + d
                arrived(first_wide.at[flat], wide_recv.at[flat])
    for _, down in along:
        for o in range(wide):
            @pl.when(o == a)
            def _(down=down, o=o):
                flat = (down - 1) * wide + o
                arrived(first_deep.at[flat], deep_recv.at[flat])

    def finish_first(i, _):
        columns = at(i * tile, tile)
        top = first_tile(row, 0, columns)
        for over, _ in across:
            top += first_wide[(over - 1) * deep + b, :, columns].astype(jnp.float32)
        for _, down in along:
            top += deep_sum[down - 1, :, columns].astype(jnp.float32)
        first_out[half(0), columns] = top.astype(jnp.bfloat16)
        low = first_tile(row, 1, columns)
        for _, down in along:
            low += first_deep[(down - 1) * wide + a, :, columns].astype(jnp.float32)
        for over, _ in across:
            low += wide_sum[over - 1, :, columns].astype(jnp.float32)
        first_out[half(1), columns] = low.astype(jnp.bfloat16)
        return 0

    lax.fori_loop(0, tiles, finish_first, 0)

    @pl.when(z != row)
    def _():
        for q in range(strips):
            for h in range(HALVES):
                arrived(second_out.at[half(h), cols(q)], spread_recv.at[q, h])
                feed(q, h).wait_send()

    def settle(t, _):
        q, i, h = split(t)

        @pl.when(jnp.logical_and(z >= row, z < rows - 1))
        def _():
            two_up(t).wait_send()

        @pl.when(jnp.logical_and(z <= row, z > 0))
        def _():
            two_down(t).wait_send()

        @pl.when(z < row)
        def _():
            chain_up(t).wait_send()

        @pl.when(z > row)
        def _():
            chain_down(t).wait_send()

        @pl.when(jnp.logical_and(home, i != rows - 1))
        def _():
            spread(t).wait_send()

        return 0

    lax.fori_loop(0, pieces, settle, 0)
    for q in range(strips):
        two_swap(q).wait_send()
        theirs_swap(q).wait_send()
    weights_swap().wait_send()
    for h in range(HALVES):
        for over, down in across + along:
            one_copy(row, h, block_of(over, down)).wait_send()
        for block in range(rows):
            one_swap(block, h).wait_send()
    for over, down in across:
        for _, other_down in along:
            one_copy(block_of(over, down), 0, block_of(0, other_down)).wait_send()
    for over, down in along:
        for other_over, _ in across:
            one_copy(block_of(over, down), 1, block_of(other_over, 0)).wait_send()

    def settle_first(u, _):
        h, over, down, target = unit(u)
        arrived(first_sent.at[target, half(h)], first_send.at[u])
        return 0

    lax.fori_loop(0, opening + closing, settle_first, 0)


def per_device(view_one, view_two, pair_weights):
    rows = lax.axis_size("row")
    samples, width = view_one.shape
    strip = min(width, 256)
    strips = width // strip
    wide, deep = PAIR, rows // PAIR
    part = samples // HALVES
    pieces = strips * rows * HALVES
    units = 2 * rows
    own = jax.ShapeDtypeStruct((samples, width), jnp.bfloat16)
    any_space = pl.BlockSpec(memory_space=pl.ANY)
    vmem = pl.BlockSpec(memory_space=pltpu.VMEM)
    dma = pltpu.SemaphoreType.DMA

    def held(*shape):
        return pltpu.VMEM(shape, jnp.bfloat16)

    crossing = (wide - 1) * deep
    descent = (deep - 1) * wide
    return pl.pallas_call(
        lambda *refs: step_kernel(rows, strip, *refs),
        out_shape=(own, own),
        in_specs=[any_space] * 3,
        out_specs=(vmem, vmem),
        scratch_shapes=[
            held(samples, width),
            held(rows, samples, width),
            held(rows, samples, width),
            held(strip, rows * samples),
            held(CORES, rows, samples, width),
            held(CORES, width, width),
            held(CORES, width, width),
            held(width, width),
            held(pieces, part, strip),
            held(pieces, part, strip),
            held(pieces, part, strip),
            pltpu.VMEM((part, strip), jnp.float32),
            held(rows, samples, width),
            held(crossing, part, width),
            held(descent, part, width),
            held(wide - 1, part, width),
            held(deep - 1, part, width),
            dma((3,)),
            dma((pieces,)),
            dma((strips, HALVES)),
            dma((pieces,)),
            dma((pieces,)),
            dma((2, strips)),
            dma((rows, HALVES, rows)),
            dma((rows, HALVES)),
            dma((2, rows, HALVES)),
            dma((2,)),
            dma((2, strips)),
            dma((pieces,)),
            dma((pieces,)),
            dma((pieces,)),
            dma((pieces,)),
            dma((strips, HALVES)),
            dma((units,)),
            dma((crossing,)),
            dma((descent,)),
            dma((wide - 1,)),
            dma((deep - 1,)),
        ],
        compiler_params=pltpu.CompilerParams(has_side_effects=True, vmem_limit_bytes=62 * 2**20),
        name="twins_step",
    )(view_one, view_two, pair_weights)


def solution(mesh):
    placed = (P("row", "col"), P("row", "col"), P("row", "col"))
    return jax.shard_map(
        per_device,
        mesh=mesh,
        in_specs=placed,
        out_specs=(P("row", "col"), P("row", "col")),
        check_vma=False,
    )
```

time: 236 us -> 219 us (0.928)
  matrix products: 16.4 us -> 0 us
    dot_general x1 -> x0, matrix products: 16.4 us -> none  [per_device(): lax.dot_general(two_rows, one_pair[:, :local_cols], (((0,), (0,)), ((), (...]
    pallas_call x2 -> x1, Pallas kernels: 214 us -> 213 us  [per_device(): pl.pallas_call(lambda *refs: step_kernel(rows, strip, *refs), out_shape=(...]
where the time goes in v1:
time: 219 us; the launch traced here: 218 us
  Pallas kernels  213 us (97%)
  local copies, waits for them, and re-layouts  4.52 us (2%)
    pallas_call x1, Pallas kernels, per_device(): pl.pallas_call(lambda *refs: step_kernel(rows, strip, *refs), out_shape=(...  213 us
    unnamed x2, local copies, waits for them, and re-layouts  4.52 us

profile of v1, /device:TPU:0, one launch (start us, length us, event | category | flops | bytes accessed | tf_op | source)
XLA Modules:
  0.0 218.4 jit_solution(8534644161662438717)
XLA Ops:
  0.6 213.2 %twins_step.1 = (bf16[512,1024]{1,0:T(8,128)(2,1)}, bf16[512,1024]{1,0:T(8,128)(2,1)}) custom-call(bf16[512,1024]{1,0:T(8,128)(2,1)} %refs_0_.1, bf16[512,1024]{1,0:T(8,128)(2,1)} %refs_1_.1, bf16[2048,1024]{1,0:T(8,128)(2,1)} %refs_2_.1), custom_call_target="tpu_custom_call" | custom-call | tf_op jit(solution)/shard_map/twins_step/pallas_call | solution.py:554
  213.9 2.3 %copy.7 = bf16[512,1024]{1,0:T(8,128)(2,1)} copy(bf16[512,1024]{1,0:T(8,128)(2,1)} %get-tuple-element.4) | data formatting | bytes 2097152
  216.1 2.3 %copy.8 = bf16[512,1024]{1,0:T(8,128)(2,1)} copy(bf16[512,1024]{1,0:T(8,128)(2,1)} %get-tuple-element.5) | data formatting | bytes 2097152

commit v2 on v1

--- a/solution.py
+++ b/solution.py
@@ -55,6 +55,7 @@
     reach = jnp.where(z > row, rows - 1 - row, jnp.where(z < row, row, jnp.maximum(row, rows - 1 - row)))
     back = reach - jnp.abs(z - row)
     last = back == 0
+    back = jnp.where(home, rows, back)
     twin = (row, col + 1 - 2 * core)
 
     def device(target, level):
@@ -139,33 +140,69 @@
 
     load_one.start()
     load_pair.start()
+
+    barrier = pltpu.get_barrier_semaphore()
+
+    def greet(target):
+        pl.semaphore_signal(barrier, inc=1, device_id=target, device_id_type=MESH)
+
+    greet(twin)
+    for step in range(1, rows):
+        greet((lax.rem(row + step, rows), col))
+
+    @pl.when(z > 0)
+    def _():
+        greet(device(row, z - 1))
+
+    @pl.when(z < rows - 1)
+    def _():
+        greet(device(row, z + 1))
+
+    pl.semaphore_wait(barrier, rows + jnp.where(z > 0, 1, 0) + jnp.where(z < rows - 1, 1, 0))
     load_two.wait()
     feeds(0)
     load_one.wait()
-    for h in range(HALVES):
-        for over, down in across:
-            one_copy(row, h, block_of(over, down)).start()
-        for over, down in along:
-            one_copy(row, HALVES - 1 - h, block_of(over, down)).start()
+    early = [(0, block_of(over, down)) for over, down in across] + [(1, block_of(over, down)) for over, down in along]
+    late = [(1, block_of(over, down)) for over, down in across] + [(0, block_of(over, down)) for over, down in along]
+    for h, target in early:
+        one_copy(row, h, target).start()
+    for h, target in late:
+        @pl.when(target != z)
+        def _(h=h, target=target):
+            one_copy(row, h, target).start()
     for h in range(HALVES):
         one_swap(row, h).start()
     weights_swap().start()
-    if strips > 1:
-        feeds(1)
+
+    def relays():
+        found = []
+        for over, down in across:
+            for _, other_down in along:
+                found.append((block_of(over, down), 0, block_of(0, other_down)))
+        for over, down in along:
+            for other_over, _ in across:
+                found.append((block_of(over, down), 1, block_of(other_over, 0)))
+        return found
 
     def relay_one():
+        if strips > 1:
+            feeds(1)
         for over, down in across:
-            block = block_of(over, down)
-            take_one(block, 0)
-            for _, other_down in along:
-                one_copy(block, 0, block_of(0, other_down)).start()
+            take_one(block_of(over, down), 0)
         for over, down in along:
-            block = block_of(over, down)
-            take_one(block, 1)
-            for other_over, _ in across:
-                one_copy(block, 1, block_of(other_over, 0)).start()
-        for q in range(2, strips):
-            feeds(q)
+            take_one(block_of(over, down), 1)
+        for block, h, target in relays():
+            @pl.when(target != z)
+            def _(block=block, h=h, target=target):
+                one_copy(block, h, target).start()
+        for h, target in late:
+            @pl.when(target == z)
+            def _(h=h, target=target):
+                one_copy(row, h, target).start()
+        for block, h, target in relays():
+            @pl.when(target == z)
+            def _(block=block, h=h, target=target):
+                one_copy(block, h, target).start()
 
     def finish_one():
         for over, down in across:
@@ -236,13 +273,11 @@
 
         keep = jnp.logical_and(home, i == rows - 1)
 
+        second_sent[g] = second_sum[...].astype(jnp.bfloat16)
+
         @pl.when(keep)
         def _():
-            second_out[half(h), cols(q)] = second_sum[...].astype(jnp.bfloat16)
-
-        @pl.when(jnp.logical_not(keep))
-        def _():
-            second_sent[g] = second_sum[...].astype(jnp.bfloat16)
+            pltpu.make_async_copy(second_sent.at[g], second_out.at[half(h), cols(q)], spread_recv.at[q, h]).start()
 
         @pl.when(z < row)
         def _():
@@ -362,14 +397,81 @@
         def _():
             wide_close(u).start()
 
+    def first_last():
+        for _, down in along:
+            arrived(deep_sum.at[down - 1], deep_last.at[down - 1])
+        for over, _ in across:
+            arrived(wide_sum.at[over - 1], wide_last.at[over - 1])
+            for d in range(deep):
+                @pl.when(d == b)
+                def _(over=over, d=d):
+                    flat = (over - 1) * deep + d
+                    arrived(first_wide.at[flat], wide_recv.at[flat])
+        for _, down in along:
+            for o in range(wide):
+                @pl.when(o == a)
+                def _(down=down, o=o):
+                    flat = (down - 1) * wide + o
+                    arrived(first_deep.at[flat], deep_recv.at[flat])
+
+        def finish_first(i, _):
+            columns = at(i * tile, tile)
+            top = first_tile(row, 0, columns)
+            for over, _ in across:
+                top += first_wide[(over - 1) * deep + b, :, columns].astype(jnp.float32)
+            for _, down in along:
+                top += deep_sum[down - 1, :, columns].astype(jnp.float32)
+            first_sent[row, half(0), columns] = top.astype(jnp.bfloat16)
+            low = first_tile(row, 1, columns)
+            for _, down in along:
+                low += first_deep[(down - 1) * wide + a, :, columns].astype(jnp.float32)
+            for over, _ in across:
+                low += wide_sum[over - 1, :, columns].astype(jnp.float32)
+            first_sent[row, half(1), columns] = low.astype(jnp.bfloat16)
+            return 0
+
+        lax.fori_loop(0, tiles, finish_first, 0)
+        pltpu.make_async_copy(first_sent.at[row], first_out, load_sem.at[3]).start()
+
     closing = len(order) - 2 - opening
-    lag = jnp.where(last, 0, jnp.minimum(6, 4 * back - 2))
+    table = list(range(chunk))
+    ends = [chunk - 1]
+    for q in range(1, strips):
+        if q <= 2:
+            owned = [1] if q == 1 else range(2, strips)
+            table += [n * chunk + h for n in owned for h in range(HALVES)]
+        table += list(range(q * chunk + HALVES, (q + 1) * chunk))
+        ends.append(len(table) - 1)
+    behind = [max(0, end - (q + 1) * chunk + 1) for q, end in enumerate(ends)]
+    shift = max(behind)
+    jump = chunk * next((q for q, late_by in enumerate(behind) if late_by), 0)
+
+    soon = back == 1
+    def starts(first_lag, later_lag, length):
+        found = []
+        for q, end in enumerate(ends):
+            begin = end + (later_lag if q else first_lag)
+            if q + 1 == strips:
+                begin = end + (length > 1)
+            found.append(max(begin, found[-1] + length) if found else begin)
+        return found
+
+    kinds = [starts(0, 0, 1), starts(4, 0, (parts + 1) // 2), starts(6, 2, parts), starts(12, 2, parts)]
+
+    def by_kind(values):
+        return jnp.where(last, values[0], jnp.where(soon, values[1], jnp.where(home, values[3], values[2])))
+
+    per = by_kind([parts, 2, 1, 1])
+    span = by_kind([1, (parts + 1) // 2, parts, parts])
     second_lag = chunk - 1 + jnp.where(last, 0, 2 + 4 * back)
-    done = jnp.where(last, pieces, pieces - 1 + lag + parts)
-    open_slot = done + 1
-    close_slot = jnp.maximum(open_slot + 2, pieces + 8 + 2 * back)
-    relay_slot = jnp.maximum(0, 4 - 2 * jnp.abs(z - row))
-    slots = pieces + chunk + 2 + 4 * rows
+    second_lag = jnp.where(home, kinds[3][0] + parts, second_lag)
+    open_slot = by_kind([kind[-1] for kind in kinds]) + 2
+    open_limit = max(kind[-1] for kind in kinds) + 3
+    close_slot = open_limit + 8 + jnp.where(home, 5, 0)
+    relay_slot = pick(jnp.abs(z - row), [8, 4, 2] + [1] * rows)
+    feed_slot = chunk + 2 - jnp.minimum(jnp.abs(z - row), 4)
+    slots = pieces + shift + 1 + max(chunk + 1 + 4 * (rows - 1), kinds[3][0] + parts)
+    last_slot = jnp.where(home, slots - 5, slots - 1)
     each = (opening + 1) // 2
 
     def slot(t, _):
@@ -377,33 +479,44 @@
         def _():
             relay_one()
 
+        for q_ in range(2, strips):
+            @pl.when(t == feed_slot + (q_ - 1) * (chunk - HALVES))
+            def _(q_=q_):
+                feeds(q_)
+
         @pl.when(t < pieces)
         def _():
-            arrived(two_piece(t), two_recv.at[t])
+            n = pick(t, table)
+            arrived(two_piece(n), two_recv.at[n])
 
             @pl.when(jnp.logical_and(z >= row, z < rows - 1))
             def _():
-                two_up(t).start()
+                two_up(n).start()
 
             @pl.when(jnp.logical_and(z <= row, z > 0))
             def _():
-                two_down(t).start()
-
-            @pl.when(lax.rem(t, chunk) == chunk - 1)
+                two_down(n).start()
+
+            @pl.when(lax.rem(n, chunk) == chunk - 1)
             def _():
-                two_swap(lax.div(t, chunk)).start()
-
-        since = t - (chunk - 1) - lag
-
-        @pl.when(since == 0)
+                two_swap(lax.div(n, chunk)).start()
+
+        @pl.when(t == by_kind([kind[0] for kind in kinds]))
         def _():
             finish_one()
 
-        q, p = lax.div(since, chunk), lax.rem(since, chunk)
-        live = jnp.logical_and(since >= 0, q < strips)
-        low = jnp.where(jnp.logical_or(last, jnp.logical_not(live)), 0, p)
-        high = jnp.where(last, jnp.where(p == 0, parts, 0), jnp.where(p < parts, p + 1, 0))
-        high = jnp.where(live, high, 0)
+        q, low, high = jnp.int32(0), jnp.int32(0), jnp.int32(0)
+        for q_ in range(strips - 1):
+            since = t - by_kind([kind[q_] for kind in kinds])
+            live = jnp.logical_and(since >= 0, since < span)
+            q = jnp.where(live, q_, q)
+            low = jnp.where(live, since * per, low)
+            high = jnp.where(live, jnp.minimum(since * per + per, parts), high)
+
+        final = t == by_kind([kind[-1] for kind in kinds])
+        q = jnp.where(final, strips - 1, q)
+        low = jnp.where(final, 0, low)
+        high = jnp.where(final, parts, high)
 
         def piece(i, _):
             correlate(q, i)
@@ -418,6 +531,7 @@
                 arrived(theirs.at[cols(q_)], theirs_sem.at[1, q_])
 
         g = t - second_lag
+        g = jnp.where(jnp.logical_or(g < jump, jnp.logical_not(last)), g, jnp.where(g < jump + shift, -1, g - shift))
 
         @pl.when(jnp.logical_and(g >= 0, g < pieces))
         def _():
@@ -437,50 +551,24 @@
             return 0
 
         lax.fori_loop(opening, jnp.where(t == close_slot, opening + closing, opening), closer, 0)
+
+        @pl.when(t == last_slot)
+        def _():
+            first_last()
+
         return 0
 
     lax.fori_loop(0, slots, slot, 0)
 
-    for _, down in along:
-        arrived(deep_sum.at[down - 1], deep_last.at[down - 1])
-    for over, _ in across:
-        arrived(wide_sum.at[over - 1], wide_last.at[over - 1])
-        for d in range(deep):
-            @pl.when(d == b)
-            def _(over=over, d=d):
-                flat = (over - 1) * deep + d
-                arrived(first_wide.at[flat], wide_recv.at[flat])
-    for _, down in along:
-        for o in range(wide):
-            @pl.when(o == a)
-            def _(down=down, o=o):
-                flat = (down - 1) * wide + o
-                arrived(first_deep.at[flat], deep_recv.at[flat])
-
-    def finish_first(i, _):
-        columns = at(i * tile, tile)
-        top = first_tile(row, 0, columns)
-        for over, _ in across:
-            top += first_wide[(over - 1) * deep + b, :, columns].astype(jnp.float32)
-        for _, down in along:
-            top += deep_sum[down - 1, :, columns].astype(jnp.float32)
-        first_out[half(0), columns] = top.astype(jnp.bfloat16)
-        low = first_tile(row, 1, columns)
-        for _, down in along:
-            low += first_deep[(down - 1) * wide + a, :, columns].astype(jnp.float32)
-        for over, _ in across:
-            low += wide_sum[over - 1, :, columns].astype(jnp.float32)
-        first_out[half(1), columns] = low.astype(jnp.bfloat16)
-        return 0
-
-    lax.fori_loop(0, tiles, finish_first, 0)
-
-    @pl.when(z != row)
-    def _():
-        for q in range(strips):
-            for h in range(HALVES):
-                arrived(second_out.at[half(h), cols(q)], spread_recv.at[q, h])
+    for q in range(strips):
+        for h in range(HALVES):
+            arrived(second_out.at[half(h), cols(q)], spread_recv.at[q, h])
+
+            @pl.when(z != row)
+            def _(q=q, h=h):
                 feed(q, h).wait_send()
+
+    arrived(first_out, load_sem.at[3])
 
     def settle(t, _):
         q, i, h = split(t)
@@ -517,12 +605,8 @@
             one_copy(row, h, block_of(over, down)).wait_send()
         for block in range(rows):
             one_swap(block, h).wait_send()
-    for over, down in across:
-        for _, other_down in along:
-            one_copy(block_of(over, down), 0, block_of(0, other_down)).wait_send()
-    for over, down in along:
-        for other_over, _ in across:
-            one_copy(block_of(over, down), 1, block_of(other_over, 0)).wait_send()
+    for block, h, target in relays():
+        one_copy(block, h, target).wait_send()
 
     def settle_first(u, _):
         h, over, down, target = unit(u)
@@ -543,7 +627,6 @@
     units = 2 * rows
     own = jax.ShapeDtypeStruct((samples, width), jnp.bfloat16)
     any_space = pl.BlockSpec(memory_space=pl.ANY)
-    vmem = pl.BlockSpec(memory_space=pltpu.VMEM)
     dma = pltpu.SemaphoreType.DMA
 
     def held(*shape):
@@ -555,7 +638,7 @@
         lambda *refs: step_kernel(rows, strip, *refs),
         out_shape=(own, own),
         in_specs=[any_space] * 3,
-        out_specs=(vmem, vmem),
+        out_specs=(any_space, any_space),
         scratch_shapes=[
             held(samples, width),
             held(rows, samples, width),
@@ -574,7 +657,7 @@
             held(descent, part, width),
             held(wide - 1, part, width),
             held(deep - 1, part, width),
-            dma((3,)),
+            dma((4,)),
             dma((pieces,)),
             dma((strips, HALVES)),
             dma((pieces,)),
@@ -596,7 +679,7 @@
             dma((wide - 1,)),
             dma((deep - 1,)),
         ],
-        compiler_params=pltpu.CompilerParams(has_side_effects=True, vmem_limit_bytes=62 * 2**20),
+        compiler_params=pltpu.CompilerParams(collective_id=0, has_side_effects=True, vmem_limit_bytes=62 * 2**20),
         name="twins_step",
     )(view_one, view_two, pair_weights)
 

time: 219 us -> 178 us (0.81)
  the two profiles are of different devices: /device:TPU:0 before, /device:TPU:19 now
where the time goes in v2:
time: 178 us
  Pallas kernels  173 us (97%)
  local copies, waits for them, and re-layouts  4.52 us (3%)
    pallas_call x1, Pallas kernels, per_device(): pl.pallas_call(lambda *refs: step_kernel(rows, strip, *refs), out_shape=(...  173 us
    unnamed x2, local copies, waits for them, and re-layouts  4.52 us

profile of v2, /device:TPU:19, one launch (start us, length us, event | category | flops | bytes accessed | tf_op | source)
XLA Modules:
  0.0 178.1 jit_solution(15226169745697773977)
XLA Ops:
  0.6 172.9 %twins_step.1 = (bf16[512,1024]{1,0:T(8,128)(2,1)}, bf16[512,1024]{1,0:T(8,128)(2,1)}) custom-call(bf16[512,1024]{1,0:T(8,128)(2,1)} %refs_0_.1, bf16[512,1024]{1,0:T(8,128)(2,1)} %refs_1_.1, bf16[2048,1024]{1,0:T(8,128)(2,1)} %refs_2_.1), custom_call_target="tpu_custom_call" | custom-call | tf_op jit(solution)/shard_map/twins_step/pallas_call | solution.py:637
  173.5 2.3 %copy.7 = bf16[512,1024]{1,0:T(8,128)(2,1)} copy(bf16[512,1024]{1,0:T(8,128)(2,1)} %get-tuple-element.4) | data formatting | bytes 2097152
  175.8 2.3 %copy.8 = bf16[512,1024]{1,0:T(8,128)(2,1)} copy(bf16[512,1024]{1,0:T(8,128)(2,1)} %get-tuple-element.5) | data formatting | bytes 2097152

commit v3 on v2

--- a/solution.py
+++ b/solution.py
@@ -55,7 +55,7 @@
     reach = jnp.where(z > row, rows - 1 - row, jnp.where(z < row, row, jnp.maximum(row, rows - 1 - row)))
     back = reach - jnp.abs(z - row)
     last = back == 0
-    back = jnp.where(home, rows, back)
+    back = rows - 1 - jnp.abs(z - row)
     twin = (row, col + 1 - 2 * core)
 
     def device(target, level):
@@ -70,9 +70,21 @@
     def split(t):
         return lax.div(t, chunk), lax.rem(lax.div(t, HALVES), rows), lax.rem(t, HALVES)
 
+    across = [(over, 0) for over in range(1, wide)]
+    along = [(0, down) for down in range(1, deep)]
+    far = [(over, down) for over in range(1, wide) for down in range(1, deep)]
+    sources = [(0, 0)] + along + far + across
+    targets = far + across + along + [(0, 0)]
+
+    def block_of(over, down):
+        return lax.rem(b + down, deep) * wide + lax.rem(a + over, wide)
+
+    def choose(i, pairs):
+        return block_of(pick(i, [over for over, _ in pairs]), pick(i, [down for _, down in pairs]))
+
     def two_piece(t):
         q, i, h = split(t)
-        return two_own.at[lax.rem(row + i, rows), half(h), cols(q)]
+        return two_own.at[choose(i, sources), half(h), cols(q)]
 
     def two_up(t):
         return remote(two_piece(t), two_piece(t), up_send.at[t], two_recv.at[t], device(row, z + 1))
@@ -81,7 +93,10 @@
         return remote(two_piece(t), two_piece(t), down_send.at[t], two_recv.at[t], device(row, z - 1))
 
     def feed(q, h):
-        t = q * chunk + lax.rem(row - z + rows, rows) * HALVES + h
+        over = lax.rem(a - lax.rem(z, wide) + wide, wide)
+        down = lax.rem(b - lax.div(z, wide) + deep, deep)
+        place = pick(over * deep + down, [sources.index((o, d)) for o in range(wide) for d in range(deep)])
+        t = q * chunk + place * HALVES + h
         return remote(two_held.at[half(h), cols(q)], two_own.at[row, half(h), cols(q)], feed_send.at[q, h],
                       two_recv.at[t], device(z, z))
 
@@ -108,13 +123,6 @@
     def one_swap(block, h):
         return remote(one_block(block, h), one_block(block, h), one_pair.at[0, block, h], one_pair.at[1, block, h],
                       twin)
-
-    def block_of(over, down):
-        return lax.rem(b + down, deep) * wide + lax.rem(a + over, wide)
-
-    across = [(over, 0) for over in range(1, wide)]
-    along = [(0, down) for down in range(1, deep)]
-    far = [(over, down) for over in range(1, wide) for down in range(1, deep)]
 
     def take_one(block, h):
         arrived(one_block(block, h), one_recv.at[block, h])
@@ -178,10 +186,20 @@
         found = []
         for over, down in across:
             for _, other_down in along:
-                found.append((block_of(over, down), 0, block_of(0, other_down)))
+                target = block_of(0, other_down)
+                found.append((block_of(over, down), 0, target, target != z))
         for over, down in along:
             for other_over, _ in across:
-                found.append((block_of(over, down), 1, block_of(other_over, 0)))
+                target = block_of(other_over, 0)
+                found.append((block_of(over, down), 1, target, True))
+        return found
+
+    def late_relays():
+        found = []
+        for over, down in along:
+            for other_over, _ in across:
+                target = block_of(other_over, 0)
+                found.append((block_of(over, down), 0, target, target == z))
         return found
 
     def relay_one():
@@ -191,16 +209,16 @@
             take_one(block_of(over, down), 0)
         for over, down in along:
             take_one(block_of(over, down), 1)
-        for block, h, target in relays():
-            @pl.when(target != z)
+        for block, h, target, live in relays():
+            @pl.when(jnp.logical_and(live, target != z))
             def _(block=block, h=h, target=target):
                 one_copy(block, h, target).start()
         for h, target in late:
             @pl.when(target == z)
             def _(h=h, target=target):
                 one_copy(row, h, target).start()
-        for block, h, target in relays():
-            @pl.when(target == z)
+        for block, h, target, live in relays():
+            @pl.when(jnp.logical_and(live, target == z))
             def _(block=block, h=h, target=target):
                 one_copy(block, h, target).start()
 
@@ -209,6 +227,10 @@
             take_one(block_of(over, down), 1)
         for over, down in along:
             take_one(block_of(over, down), 0)
+        for block, h, target, live in late_relays():
+            @pl.when(live)
+            def _(block=block, h=h, target=target):
+                one_copy(block, h, target).start()
         for over, down in far:
             take_one(block_of(over, down), 0)
             take_one(block_of(over, down), 1)
@@ -247,14 +269,14 @@
     def spread(g):
         q, i, h = split(g)
         return remote(second_sent.at[g], second_out.at[half(h), cols(q)], spread_send.at[g], spread_recv.at[q, h],
-                      device(lax.rem(row + 1 + i, rows), z))
+                      device(choose(i, targets), z))
 
     from_below = jnp.logical_and(z > 0, z <= row)
     from_above = jnp.logical_and(z < rows - 1, z >= row)
 
     def second_piece(g):
         q, i, h = split(g)
-        target = lax.rem(row + 1 + i, rows)
+        target = choose(i, targets)
         contract = (((1,), (1,)), ((), ()))
         second_sum[...] = (
             lax.dot_general(one[0, target, half(h)], weighted[0, cols(q)], contract, preferred_element_type=jnp.float32)
@@ -434,19 +456,19 @@
         pltpu.make_async_copy(first_sent.at[row], first_out, load_sem.at[3]).start()
 
     closing = len(order) - 2 - opening
-    table = list(range(chunk))
+    def run(q, order):
+        return [q * chunk + sources.index(pair) * HALVES + h for pair in order for h in range(HALVES)]
+
+    table = run(0, [(0, 0)] + across + along + far)
     ends = [chunk - 1]
     for q in range(1, strips):
         if q <= 2:
-            owned = [1] if q == 1 else range(2, strips)
-            table += [n * chunk + h for n in owned for h in range(HALVES)]
-        table += list(range(q * chunk + HALVES, (q + 1) * chunk))
+            for owned in [1] if q == 1 else range(2, strips):
+                table += run(owned, [(0, 0)])
+        table += run(q, sources[1:])
         ends.append(len(table) - 1)
-    behind = [max(0, end - (q + 1) * chunk + 1) for q, end in enumerate(ends)]
-    shift = max(behind)
-    jump = chunk * next((q for q, late_by in enumerate(behind) if late_by), 0)
-
-    soon = back == 1
+    shift = max(end - (q + 1) * chunk + 1 for q, end in enumerate(ends))
+    soon = jnp.logical_and(back == 1, jnp.logical_not(last))
     def starts(first_lag, later_lag, length):
         found = []
         for q, end in enumerate(ends):
@@ -456,22 +478,23 @@
             found.append(max(begin, found[-1] + length) if found else begin)
         return found
 
-    kinds = [starts(0, 0, 1), starts(4, 0, (parts + 1) // 2), starts(6, 2, parts), starts(12, 2, parts)]
+    kinds = [starts(0, 0, 1), starts(4, 0, (parts + 1) // 2), starts(6, 2, parts), starts(13, 2, parts)]
 
     def by_kind(values):
         return jnp.where(last, values[0], jnp.where(soon, values[1], jnp.where(home, values[3], values[2])))
 
     per = by_kind([parts, 2, 1, 1])
     span = by_kind([1, (parts + 1) // 2, parts, parts])
-    second_lag = chunk - 1 + jnp.where(last, 0, 2 + 4 * back)
-    second_lag = jnp.where(home, kinds[3][0] + parts, second_lag)
+    home_lag = max(kinds[3][0] + parts, chunk + 1 + 4 * (rows - 1))
+    second_lag = jnp.where(last, chunk - 1, jnp.where(home, home_lag, chunk + 1 + 4 * back))
+    second_slot = by_kind([kind[0] for kind in kinds]) + jnp.where(last, 0, span)
     open_slot = by_kind([kind[-1] for kind in kinds]) + 2
     open_limit = max(kind[-1] for kind in kinds) + 3
-    close_slot = open_limit + 8 + jnp.where(home, 5, 0)
+    close_slot = open_limit + by_kind([6, 6, 8, 12])
     relay_slot = pick(jnp.abs(z - row), [8, 4, 2] + [1] * rows)
-    feed_slot = chunk + 2 - jnp.minimum(jnp.abs(z - row), 4)
-    slots = pieces + shift + 1 + max(chunk + 1 + 4 * (rows - 1), kinds[3][0] + parts)
-    last_slot = jnp.where(home, slots - 5, slots - 1)
+    feed_slot = chunk + 1 - jnp.minimum(jnp.abs(z - row), 4)
+    slots = pieces + 1 + home_lag + shift
+    last_slot = slots - 1
     each = (opening + 1) // 2
 
     def slot(t, _):
@@ -480,7 +503,7 @@
             relay_one()
 
         for q_ in range(2, strips):
-            @pl.when(t == feed_slot + (q_ - 1) * (chunk - HALVES))
+            @pl.when(t == feed_slot + (q_ - 2) * (chunk - HALVES))
             def _(q_=q_):
                 feeds(q_)
 
@@ -497,9 +520,10 @@
             def _():
                 two_down(n).start()
 
-            @pl.when(lax.rem(n, chunk) == chunk - 1)
-            def _():
-                two_swap(lax.div(n, chunk)).start()
+            for q_ in range(strips):
+                @pl.when(t == ends[q_])
+                def _(q_=q_):
+                    two_swap(q_).start()
 
         @pl.when(t == by_kind([kind[0] for kind in kinds]))
         def _():
@@ -530,12 +554,17 @@
                 arrived(two_twin.at[:, :, cols(q_)], two_pair.at[1, q_])
                 arrived(theirs.at[cols(q_)], theirs_sem.at[1, q_])
 
-        g = t - second_lag
-        g = jnp.where(jnp.logical_or(g < jump, jnp.logical_not(last)), g, jnp.where(g < jump + shift, -1, g - shift))
-
-        @pl.when(jnp.logical_and(g >= 0, g < pieces))
-        def _():
+        def second_count(t):
+            ahead = t - second_lag + 1
+            count = jnp.maximum(jnp.minimum(ahead, 2 * chunk), ahead - shift)
+            count = jnp.maximum(count, jnp.where(soon, jnp.minimum(ahead + 2, chunk), 0))
+            return jnp.where(t < second_slot, 0, jnp.clip(count, 0, pieces))
+
+        def second(g, _):
             second_piece(g)
+            return 0
+
+        lax.fori_loop(second_count(t - 1), second_count(t), second, 0)
 
         first = jnp.where(t == open_slot, 0, jnp.where(t == open_slot + 1, each, opening))
         final = jnp.where(t == open_slot, each, opening)
@@ -605,8 +634,10 @@
             one_copy(row, h, block_of(over, down)).wait_send()
         for block in range(rows):
             one_swap(block, h).wait_send()
-    for block, h, target in relays():
-        one_copy(block, h, target).wait_send()
+    for block, h, target, live in relays() + late_relays():
+        @pl.when(live)
+        def _(block=block, h=h, target=target):
+            one_copy(block, h, target).wait_send()
 
     def settle_first(u, _):
         h, over, down, target = unit(u)

time: 178 us -> 172 us (0.966)
  the two profiles are of different devices: /device:TPU:19 before, /device:TPU:0 now
where the time goes in v3:
time: 172 us
  Pallas kernels  166 us (97%)
  local copies, waits for them, and re-layouts  4.52 us (3%)
    pallas_call x1, Pallas kernels, per_device(): pl.pallas_call(lambda *refs: step_kernel(rows, strip, *refs), out_shape=(...  166 us
    unnamed x2, local copies, waits for them, and re-layouts  4.52 us

profile of v3, /device:TPU:0, one launch (start us, length us, event | category | flops | bytes accessed | tf_op | source)
XLA Modules:
  0.0 171.6 jit_solution(11646921435377985847)
XLA Ops:
  0.6 166.4 %twins_step.1 = (bf16[512,1024]{1,0:T(8,128)(2,1)}, bf16[512,1024]{1,0:T(8,128)(2,1)}) custom-call(bf16[512,1024]{1,0:T(8,128)(2,1)} %refs_0_.1, bf16[512,1024]{1,0:T(8,128)(2,1)} %refs_1_.1, bf16[2048,1024]{1,0:T(8,128)(2,1)} %refs_2_.1), custom_call_target="tpu_custom_call" | custom-call | tf_op jit(solution)/shard_map/twins_step/pallas_call | solution.py:668
  167.1 2.3 %copy.7 = bf16[512,1024]{1,0:T(8,128)(2,1)} copy(bf16[512,1024]{1,0:T(8,128)(2,1)} %get-tuple-element.4) | data formatting | bytes 2097152
  169.3 2.3 %copy.8 = bf16[512,1024]{1,0:T(8,128)(2,1)} copy(bf16[512,1024]{1,0:T(8,128)(2,1)} %get-tuple-element.5) | data formatting | bytes 2097152

commit v4 on v3

--- a/solution.py
+++ b/solution.py
@@ -8,6 +8,7 @@
 MESH = pl.DeviceIdType.MESH
 CORES = 2
 HALVES = 2
+QUARTERS = 4
 PAIR = 2
 
 
@@ -34,9 +35,8 @@
 
 def step_kernel(rows, strip, one_ref, two_ref, pair_ref, first_out, second_out, two_held, two_own, two_twin, turned, one,
                 pair, weighted, theirs, below, above, second_sent, second_sum, first_sent, first_wide, first_deep,
-                wide_sum, deep_sum, load_sem, two_recv, feed_send, up_send, down_send, two_pair, one_send, one_recv,
-                one_pair, weight_sem, theirs_sem, chain_send, below_recv, above_recv, spread_send, spread_recv,
-                first_send, wide_recv, deep_recv, wide_last, deep_last):
+                wide_sum, deep_sum, first_own, load_sem, two_recv, one_send, one_recv, below_recv, above_recv, wide_recv,
+                deep_recv, wide_last, deep_last, sent, whole):
     samples, width = two_ref.shape
     wide = PAIR
     deep = rows // wide
@@ -87,17 +87,17 @@
         return two_own.at[choose(i, sources), half(h), cols(q)]
 
     def two_up(t):
-        return remote(two_piece(t), two_piece(t), up_send.at[t], two_recv.at[t], device(row, z + 1))
+        return remote(two_piece(t), two_piece(t), sent.at[0], two_recv.at[t], device(row, z + 1))
 
     def two_down(t):
-        return remote(two_piece(t), two_piece(t), down_send.at[t], two_recv.at[t], device(row, z - 1))
+        return remote(two_piece(t), two_piece(t), sent.at[1], two_recv.at[t], device(row, z - 1))
 
     def feed(q, h):
         over = lax.rem(a - lax.rem(z, wide) + wide, wide)
         down = lax.rem(b - lax.div(z, wide) + deep, deep)
         place = pick(over * deep + down, [sources.index((o, d)) for o in range(wide) for d in range(deep)])
         t = q * chunk + place * HALVES + h
-        return remote(two_held.at[half(h), cols(q)], two_own.at[row, half(h), cols(q)], feed_send.at[q, h],
+        return remote(two_held.at[half(h), cols(q)], two_own.at[row, half(h), cols(q)], sent.at[2],
                       two_recv.at[t], device(z, z))
 
     def own_two(q, h):
@@ -111,28 +111,26 @@
                 feed(q, h).start()
 
     def two_swap(q):
-        return remote(two_own.at[:, :, cols(q)], two_twin.at[:, :, cols(q)], two_pair.at[0, q], two_pair.at[1, q], twin)
+        return remote(two_own.at[:, :, cols(q)], two_twin.at[:, :, cols(q)], sent.at[3], whole.at[0], twin)
 
     def one_block(block, h):
         return one.at[core, block, half(h)]
 
-    def one_copy(block, h, target):
-        return remote(one_block(block, h), one_block(block, h), one_send.at[block, h, target], one_recv.at[block, h],
-                      (target, col))
+    def one_copy(block, h, target, send):
+        return remote(one_block(block, h), one_block(block, h), send, one_recv.at[block, h], (target, col))
 
     def one_swap(block, h):
-        return remote(one_block(block, h), one_block(block, h), one_pair.at[0, block, h], one_pair.at[1, block, h],
-                      twin)
+        return remote(one_block(block, h), one_block(block, h), sent.at[4], whole.at[1], twin)
 
     def take_one(block, h):
         arrived(one_block(block, h), one_recv.at[block, h])
         one_swap(block, h).start()
 
     def weights_swap():
-        return remote(pair_ref.at[at(other * width, width)], pair.at[core], weight_sem.at[0], weight_sem.at[1], twin)
+        return remote(pair_ref.at[at(other * width, width)], pair.at[core], sent.at[6], whole.at[3], twin)
 
     def theirs_swap(q):
-        return remote(weighted.at[other, cols(q)], theirs.at[cols(q)], theirs_sem.at[0, q], theirs_sem.at[1, q], twin)
+        return remote(weighted.at[other, cols(q)], theirs.at[cols(q)], sent.at[5], whole.at[2], twin)
 
     load_two = pltpu.make_async_copy(two_ref, two_held, load_sem.at[0])
     load_one = pltpu.make_async_copy(one_ref, one.at[core, row], load_sem.at[1])
@@ -173,11 +171,11 @@
     early = [(0, block_of(over, down)) for over, down in across] + [(1, block_of(over, down)) for over, down in along]
     late = [(1, block_of(over, down)) for over, down in across] + [(0, block_of(over, down)) for over, down in along]
     for h, target in early:
-        one_copy(row, h, target).start()
+        one_copy(row, h, target, sent.at[7]).start()
     for h, target in late:
         @pl.when(target != z)
         def _(h=h, target=target):
-            one_copy(row, h, target).start()
+            one_copy(row, h, target, sent.at[7]).start()
     for h in range(HALVES):
         one_swap(row, h).start()
     weights_swap().start()
@@ -185,22 +183,25 @@
     def relays():
         found = []
         for over, down in across:
-            for _, other_down in along:
+            for i, (_, other_down) in enumerate(along):
                 target = block_of(0, other_down)
-                found.append((block_of(over, down), 0, target, target != z))
+                found.append((block_of(over, down), 0, target, target != z, i))
         for over, down in along:
-            for other_over, _ in across:
+            for i, (other_over, _) in enumerate(across):
                 target = block_of(other_over, 0)
-                found.append((block_of(over, down), 1, target, True))
+                found.append((block_of(over, down), 1, target, True, i))
         return found
 
     def late_relays():
         found = []
         for over, down in along:
-            for other_over, _ in across:
+            for i, (other_over, _) in enumerate(across):
                 target = block_of(other_over, 0)
-                found.append((block_of(over, down), 0, target, target == z))
+                found.append((block_of(over, down), 0, target, target == z, i))
         return found
+
+    def relay(block, h, target, i):
+        return one_copy(block, h, target, one_send.at[block, h, i])
 
     def relay_one():
         if strips > 1:
@@ -209,36 +210,34 @@
             take_one(block_of(over, down), 0)
         for over, down in along:
             take_one(block_of(over, down), 1)
-        for block, h, target, live in relays():
+        for block, h, target, live, i in relays():
             @pl.when(jnp.logical_and(live, target != z))
-            def _(block=block, h=h, target=target):
-                one_copy(block, h, target).start()
+            def _(block=block, h=h, target=target, i=i):
+                relay(block, h, target, i).start()
         for h, target in late:
             @pl.when(target == z)
             def _(h=h, target=target):
-                one_copy(row, h, target).start()
-        for block, h, target, live in relays():
+                one_copy(row, h, target, sent.at[7]).start()
+        for block, h, target, live, i in relays():
             @pl.when(jnp.logical_and(live, target == z))
-            def _(block=block, h=h, target=target):
-                one_copy(block, h, target).start()
+            def _(block=block, h=h, target=target, i=i):
+                relay(block, h, target, i).start()
 
     def finish_one():
         for over, down in across:
             take_one(block_of(over, down), 1)
         for over, down in along:
             take_one(block_of(over, down), 0)
-        for block, h, target, live in late_relays():
+        for block, h, target, live, i in late_relays():
             @pl.when(live)
-            def _(block=block, h=h, target=target):
-                one_copy(block, h, target).start()
+            def _(block=block, h=h, target=target, i=i):
+                relay(block, h, target, i).start()
         for over, down in far:
             take_one(block_of(over, down), 0)
             take_one(block_of(over, down), 1)
-        for block in range(rows):
-            for h in range(HALVES):
-                arrived(one.at[other, block, half(h)], one_pair.at[1, block, h])
+        arrived(one.at[other], whole.at[1])
         load_pair.wait()
-        arrived(pair.at[other], weight_sem.at[1])
+        arrived(pair.at[other], whole.at[3])
 
     def correlate(q, p):
         side, i = lax.div(p, tiles), lax.rem(p, tiles)
@@ -261,14 +260,14 @@
             theirs_swap(q).start()
 
     def chain_up(g):
-        return remote(second_sent.at[g], below.at[g], chain_send.at[g], below_recv.at[g], device(row, z + 1))
+        return remote(second_sent.at[g], below.at[g], sent.at[8], below_recv.at[g], device(row, z + 1))
 
     def chain_down(g):
-        return remote(second_sent.at[g], above.at[g], chain_send.at[g], above_recv.at[g], device(row, z - 1))
+        return remote(second_sent.at[g], above.at[g], sent.at[8], above_recv.at[g], device(row, z - 1))
 
     def spread(g):
         q, i, h = split(g)
-        return remote(second_sent.at[g], second_out.at[half(h), cols(q)], spread_send.at[g], spread_recv.at[q, h],
+        return remote(second_sent.at[g], second_out.at[half(h), cols(q)], sent.at[9], whole.at[4],
                       device(choose(i, targets), z))
 
     from_below = jnp.logical_and(z > 0, z <= row)
@@ -299,7 +298,7 @@
 
         @pl.when(keep)
         def _():
-            pltpu.make_async_copy(second_sent.at[g], second_out.at[half(h), cols(q)], spread_recv.at[q, h]).start()
+            pltpu.make_async_copy(second_sent.at[g], second_out.at[half(h), cols(q)], whole.at[4]).start()
 
         @pl.when(z < row)
         def _():
@@ -334,22 +333,22 @@
 
     def wide_open(u):
         h, over, down, target, flat = first_hop(u)
-        return remote(first_sent.at[target, half(h)], first_wide.at[flat], first_send.at[u], wide_recv.at[flat],
+        return remote(first_sent.at[target, half(h)], first_wide.at[flat], sent.at[10], wide_recv.at[flat],
                       (b * wide + lax.rem(a + over, wide), col))
 
     def deep_open(u):
         h, over, down, target, flat = first_hop(u)
-        return remote(first_sent.at[target, half(h)], first_deep.at[flat], first_send.at[u], deep_recv.at[flat],
+        return remote(first_sent.at[target, half(h)], first_deep.at[flat], sent.at[10], deep_recv.at[flat],
                       (lax.rem(b + down, deep) * wide + a, col))
 
     def deep_close(u):
         h, over, down, target = unit(u)
-        return remote(first_sent.at[target, half(h)], deep_sum.at[down - 1], first_send.at[u], deep_last.at[down - 1],
+        return remote(first_sent.at[target, half(h)], deep_sum.at[down - 1], sent.at[10], deep_last.at[down - 1],
                       (target, col))
 
     def wide_close(u):
         h, over, down, target = unit(u)
-        return remote(first_sent.at[target, half(h)], wide_sum.at[over - 1], first_send.at[u], wide_last.at[over - 1],
+        return remote(first_sent.at[target, half(h)], wide_sum.at[over - 1], sent.at[10], wide_last.at[over - 1],
                       (target, col))
 
     def first_tile(target, h, columns):
@@ -438,13 +437,13 @@
 
         def finish_first(i, _):
             columns = at(i * tile, tile)
-            top = first_tile(row, 0, columns)
+            top = first_own[half(0), columns]
             for over, _ in across:
                 top += first_wide[(over - 1) * deep + b, :, columns].astype(jnp.float32)
             for _, down in along:
                 top += deep_sum[down - 1, :, columns].astype(jnp.float32)
             first_sent[row, half(0), columns] = top.astype(jnp.bfloat16)
-            low = first_tile(row, 1, columns)
+            low = first_own[half(1), columns]
             for _, down in along:
                 low += first_deep[(down - 1) * wide + a, :, columns].astype(jnp.float32)
             for over, _ in across:
@@ -489,7 +488,7 @@
     second_lag = jnp.where(last, chunk - 1, jnp.where(home, home_lag, chunk + 1 + 4 * back))
     second_slot = by_kind([kind[0] for kind in kinds]) + jnp.where(last, 0, span)
     open_slot = by_kind([kind[-1] for kind in kinds]) + 2
-    open_limit = max(kind[-1] for kind in kinds) + 3
+    open_limit = max(kind[-1] for kind in kinds) + 1 + opening
     close_slot = open_limit + by_kind([6, 6, 8, 12])
     relay_slot = pick(jnp.abs(z - row), [8, 4, 2] + [1] * rows)
     feed_slot = chunk + 1 - jnp.minimum(jnp.abs(z - row), 4)
@@ -550,9 +549,8 @@
 
         @pl.when(t == open_slot)
         def _():
-            for q_ in range(strips):
-                arrived(two_twin.at[:, :, cols(q_)], two_pair.at[1, q_])
-                arrived(theirs.at[cols(q_)], theirs_sem.at[1, q_])
+            arrived(two_twin, whole.at[0])
+            arrived(theirs, whole.at[2])
 
         def second_count(t):
             ahead = t - second_lag + 1
@@ -566,8 +564,9 @@
 
         lax.fori_loop(second_count(t - 1), second_count(t), second, 0)
 
-        first = jnp.where(t == open_slot, 0, jnp.where(t == open_slot + 1, each, opening))
-        final = jnp.where(t == open_slot, each, opening)
+        turn = t - open_slot
+        first = jnp.where(turn > 0, turn + 1, 0)
+        final = jnp.where(jnp.logical_and(turn >= 0, turn < opening - 1), turn + 2, first)
 
         def opener(u, _):
             first_opening(u)
@@ -579,7 +578,16 @@
             first_closing(u)
             return 0
 
-        lax.fori_loop(opening, jnp.where(t == close_slot, opening + closing, opening), closer, 0)
+        turn = t - close_slot
+        first = opening + turn
+        final = jnp.where(jnp.logical_and(turn >= 0, turn < closing), first + 1, first)
+        lax.fori_loop(first, final, closer, 0)
+        turn = t - open_slot - opening
+
+        @pl.when(jnp.logical_and(turn >= 0, turn < HALVES * tiles))
+        def _():
+            h, columns = lax.div(turn, tiles), at(lax.rem(turn, tiles) * tile, tile)
+            first_own[half(h), columns] = first_tile(row, h, columns)
 
         @pl.when(t == last_slot)
         def _():
@@ -589,62 +597,71 @@
 
     lax.fori_loop(0, slots, slot, 0)
 
-    for q in range(strips):
-        for h in range(HALVES):
-            arrived(second_out.at[half(h), cols(q)], spread_recv.at[q, h])
-
-            @pl.when(z != row)
-            def _(q=q, h=h):
-                feed(q, h).wait_send()
-
+    arrived(second_out, whole.at[4])
     arrived(first_out, load_sem.at[3])
 
-    def settle(t, _):
-        q, i, h = split(t)
-
-        @pl.when(jnp.logical_and(z >= row, z < rows - 1))
-        def _():
-            two_up(t).wait_send()
-
-        @pl.when(jnp.logical_and(z <= row, z > 0))
-        def _():
-            two_down(t).wait_send()
-
-        @pl.when(z < row)
-        def _():
-            chain_up(t).wait_send()
-
-        @pl.when(z > row)
-        def _():
-            chain_down(t).wait_send()
-
-        @pl.when(jnp.logical_and(home, i != rows - 1))
-        def _():
-            spread(t).wait_send()
-
-        return 0
-
-    lax.fori_loop(0, pieces, settle, 0)
-    for q in range(strips):
-        two_swap(q).wait_send()
-        theirs_swap(q).wait_send()
-    weights_swap().wait_send()
-    for h in range(HALVES):
-        for over, down in across + along:
-            one_copy(row, h, block_of(over, down)).wait_send()
-        for block in range(rows):
-            one_swap(block, h).wait_send()
-    for block, h, target, live in relays() + late_relays():
+    @pl.when(z != row)
+    def _():
+        arrived(two_held, sent.at[2])
+        arrived(second_sent, sent.at[8])
+
+    @pl.when(home)
+    def _():
+        arrived(second_sent.at[pl.ds(0, pieces - strips * HALVES)], sent.at[9])
+
+    @pl.when(jnp.logical_and(z >= row, z < rows - 1))
+    def _():
+        arrived(two_own, sent.at[0])
+
+    @pl.when(jnp.logical_and(z <= row, z > 0))
+    def _():
+        arrived(two_own, sent.at[1])
+
+    arrived(two_own, sent.at[3])
+    arrived(one.at[core], sent.at[4])
+    arrived(weighted.at[other], sent.at[5])
+    arrived(pair.at[core], sent.at[6])
+    arrived(one.at[core, pl.ds(0, len(across + along))], sent.at[7])
+    for block, h, target, live, i in relays() + late_relays():
         @pl.when(live)
-        def _(block=block, h=h, target=target):
-            one_copy(block, h, target).wait_send()
-
-    def settle_first(u, _):
-        h, over, down, target = unit(u)
-        arrived(first_sent.at[target, half(h)], first_send.at[u])
-        return 0
-
-    lax.fori_loop(0, opening + closing, settle_first, 0)
+        def _(block=block, h=h, target=target, i=i):
+            relay(block, h, target, i).wait_send()
+
+    arrived(first_sent.at[pl.ds(0, rows - 1)], sent.at[10])
+
+
+def settle_kernel(first_ref, second_ref, first_out, second_out, first, second, load, store):
+    pairs = ((first_ref, first, first_out), (second_ref, second, second_out))
+    part = first_ref.shape[0] // QUARTERS
+
+    def copy(which, i, out):
+        source, held, target = pairs[which]
+        here = pl.ds(i * part, part)
+        if out:
+            return pltpu.make_async_copy(held.at[here], target.at[here], store.at[which, i])
+        return pltpu.make_async_copy(source.at[here], held.at[here], load.at[which, i])
+
+    order = [(which, i) for i in range(QUARTERS) for which in range(2)]
+    for which, i in order:
+        copy(which, i, False).start()
+    for which, i in order:
+        copy(which, i, False).wait()
+        copy(which, i, True).start()
+    for which, i in order:
+        copy(which, i, True).wait()
+
+
+def settle(first, second):
+    any_space = pl.BlockSpec(memory_space=pl.ANY)
+    dma = pltpu.SemaphoreType.DMA
+    return pl.pallas_call(
+        settle_kernel,
+        out_shape=[jax.ShapeDtypeStruct(x.shape, x.dtype) for x in (first, second)],
+        in_specs=[any_space] * 2,
+        out_specs=[any_space] * 2,
+        scratch_shapes=[pltpu.VMEM(x.shape, x.dtype) for x in (first, second)] + [dma((2, QUARTERS))] * 2,
+        name="settle_grads",
+    )(first, second)
 
 
 def per_device(view_one, view_two, pair_weights):
@@ -655,7 +672,6 @@
     wide, deep = PAIR, rows // PAIR
     part = samples // HALVES
     pieces = strips * rows * HALVES
-    units = 2 * rows
     own = jax.ShapeDtypeStruct((samples, width), jnp.bfloat16)
     any_space = pl.BlockSpec(memory_space=pl.ANY)
     dma = pltpu.SemaphoreType.DMA
@@ -665,7 +681,7 @@
 
     crossing = (wide - 1) * deep
     descent = (deep - 1) * wide
-    return pl.pallas_call(
+    first, second = pl.pallas_call(
         lambda *refs: step_kernel(rows, strip, *refs),
         out_shape=(own, own),
         in_specs=[any_space] * 3,
@@ -688,31 +704,24 @@
             held(descent, part, width),
             held(wide - 1, part, width),
             held(deep - 1, part, width),
+            pltpu.VMEM((samples, width), jnp.float32),
             dma((4,)),
             dma((pieces,)),
-            dma((strips, HALVES)),
+            dma((rows, HALVES, max(wide, deep) - 1)),
+            dma((rows, HALVES)),
             dma((pieces,)),
             dma((pieces,)),
-            dma((2, strips)),
-            dma((rows, HALVES, rows)),
-            dma((rows, HALVES)),
-            dma((2, rows, HALVES)),
-            dma((2,)),
-            dma((2, strips)),
-            dma((pieces,)),
-            dma((pieces,)),
-            dma((pieces,)),
-            dma((pieces,)),
-            dma((strips, HALVES)),
-            dma((units,)),
             dma((crossing,)),
             dma((descent,)),
             dma((wide - 1,)),
             dma((deep - 1,)),
+            dma((11,)),
+            dma((5,)),
         ],
         compiler_params=pltpu.CompilerParams(collective_id=0, has_side_effects=True, vmem_limit_bytes=62 * 2**20),
         name="twins_step",
     )(view_one, view_two, pair_weights)
+    return settle(first, second)
 
 
 def solution(mesh):

time: 172 us -> 166 us (0.965)
  local copies, waits for them, and re-layouts: 4.52 us -> 0 us
    unnamed x2 -> x0, local copies, waits for them, and re-layouts: 4.52 us -> none
    pallas_call x1, Pallas kernels: 166 us -> 163 us  [per_device(): pl.pallas_call(lambda *refs: step_kernel(rows, strip, *refs), out_shape=(...]
    pallas_call x0 -> x1, Pallas kernels: none -> 2.39 us  [settle(): pl.pallas_call(settle_kernel, out_shape=[jax.ShapeDtypeStruct(x.shape, x....]
where the time goes in v4:
time: 166 us
  Pallas kernels  165 us (99%)
    pallas_call x1, Pallas kernels, per_device(): pl.pallas_call(lambda *refs: step_kernel(rows, strip, *refs), out_shape=(...  163 us

profile of v4, /device:TPU:0, one launch (start us, length us, event | category | flops | bytes accessed | tf_op | source)
XLA Modules:
  0.0 166.0 jit_solution(3748757769978887555)
XLA Ops:
  0.6 163.0 %twins_step.1 = (bf16[512,1024]{1,0:T(8,128)(2,1)}, bf16[512,1024]{1,0:T(8,128)(2,1)}) custom-call(bf16[512,1024]{1,0:T(8,128)(2,1)} %refs_0_.1, bf16[512,1024]{1,0:T(8,128)(2,1)} %refs_1_.1, bf16[2048,1024]{1,0:T(8,128)(2,1)} %refs_2_.1), custom_call_target="tpu_custom_call" | custom-call | tf_op jit(solution)/shard_map/twins_step/pallas_call | solution.py:684
  163.6 2.4 %settle_grads.1 = (bf16[512,1024]{1,0:T(8,128)(2,1)}, bf16[512,1024]{1,0:T(8,128)(2,1)}) custom-call(bf16[512,1024]{1,0:T(8,128)(2,1)} %get-tuple-element.4.first_ref, bf16[512,1024]{1,0:T(8,128)(2,1)} %get-tuple-element.5.second_ref), custom_call_target="tpu_custom_call" | custom-call | tf_op jit(solution)/shard_map/settle_grads/pallas_call | solution.py:657

commit v5 on v4

--- a/solution.py
+++ b/solution.py
@@ -35,8 +35,8 @@
 
 def step_kernel(rows, strip, one_ref, two_ref, pair_ref, first_out, second_out, two_held, two_own, two_twin, turned, one,
                 pair, weighted, theirs, below, above, second_sent, second_sum, first_sent, first_wide, first_deep,
-                wide_sum, deep_sum, first_own, load_sem, two_recv, one_send, one_recv, below_recv, above_recv, wide_recv,
-                deep_recv, wide_last, deep_last, sent, whole):
+                wide_sum, deep_sum, first_own, passing, handed, load_sem, two_recv, one_send, one_recv, below_recv, above_recv, wide_recv,
+                deep_recv, wide_last, deep_last, pass_recv, handed_recv, sent, whole):
     samples, width = two_ref.shape
     wide = PAIR
     deep = rows // wide
@@ -73,7 +73,7 @@
     across = [(over, 0) for over in range(1, wide)]
     along = [(0, down) for down in range(1, deep)]
     far = [(over, down) for over in range(1, wide) for down in range(1, deep)]
-    sources = [(0, 0)] + along + far + across
+    sources = [(0, 0)] + across + along + far
     targets = far + across + along + [(0, 0)]
 
     def block_of(over, down):
@@ -104,11 +104,47 @@
         return pltpu.make_async_copy(two_ref.at[half(h), cols(q)], two_own.at[row, half(h), cols(q)],
                                      two_recv.at[q * chunk + h])
 
+    home_a, home_b = lax.rem(z, wide), lax.div(z, wide)
+    remote_a, remote_b = a != home_a, b != home_b
+
+    home_a, home_b = lax.rem(z, wide), lax.div(z, wide)
+    remote_a, remote_b = a != home_a, b != home_b
+    opposite = jnp.logical_and(remote_a, remote_b)
+    helper = jnp.logical_and(remote_a, jnp.logical_not(remote_b))
+    detours = list(range(0, strips, 2))
+
+    def hand(q, h):
+        place = lax.rem(b - home_b + deep, deep) - 1
+        n = detours.index(q)
+        return remote(two_held.at[half(h), cols(q)], handed.at[n, place, half(h)], sent.at[2],
+                      handed_recv.at[n, place, h], device(home_b * wide + a, z))
+
+    def hand_on(q, down, h):
+        over = lax.rem(a - home_a + wide, wide)
+        place = pick(over, [sources.index((max(o, 1), down)) for o in range(wide)])
+        n = detours.index(q)
+        return remote(handed.at[n, down - 1, half(h)], two_own.at[block_of(0, down), half(h), cols(q)], sent.at[12],
+                      two_recv.at[q * chunk + place * HALVES + h], device(z, z))
+
+    def hand_over(q):
+        for _, down in along:
+            for h in range(HALVES):
+                arrived(handed.at[detours.index(q), down - 1, half(h)], handed_recv.at[detours.index(q), down - 1, h])
+                hand_on(q, down, h).start()
+
     def feeds(q):
-        @pl.when(z != row)
+        direct = jnp.logical_and(z != row, jnp.logical_not(opposite)) if q in detours else z != row
+
+        @pl.when(direct)
         def _():
             for h in range(HALVES):
                 feed(q, h).start()
+
+        if q in detours:
+            @pl.when(opposite)
+            def _():
+                for h in range(HALVES):
+                    hand(q, h).start()
 
     def two_swap(q):
         return remote(two_own.at[:, :, cols(q)], two_twin.at[:, :, cols(q)], sent.at[3], whole.at[0], twin)
@@ -166,13 +202,12 @@
 
     pl.semaphore_wait(barrier, rows + jnp.where(z > 0, 1, 0) + jnp.where(z < rows - 1, 1, 0))
     load_two.wait()
+
     feeds(0)
     load_one.wait()
     early = [(0, block_of(over, down)) for over, down in across] + [(1, block_of(over, down)) for over, down in along]
     late = [(1, block_of(over, down)) for over, down in across] + [(0, block_of(over, down)) for over, down in along]
-    for h, target in early:
-        one_copy(row, h, target, sent.at[7]).start()
-    for h, target in late:
+    for h, target in early + late:
         @pl.when(target != z)
         def _(h=h, target=target):
             one_copy(row, h, target, sent.at[7]).start()
@@ -180,24 +215,25 @@
         one_swap(row, h).start()
     weights_swap().start()
 
+    @pl.when(helper)
+    def _():
+        hand_over(0)
+
+    for h, target in early:
+        @pl.when(target == z)
+        def _(h=h, target=target):
+            one_copy(row, h, target, sent.at[7]).start()
+
     def relays():
         found = []
         for over, down in across:
             for i, (_, other_down) in enumerate(along):
                 target = block_of(0, other_down)
-                found.append((block_of(over, down), 0, target, target != z, i))
+                found.append((block_of(over, down), 0, target, i))
         for over, down in along:
             for i, (other_over, _) in enumerate(across):
                 target = block_of(other_over, 0)
-                found.append((block_of(over, down), 1, target, True, i))
-        return found
-
-    def late_relays():
-        found = []
-        for over, down in along:
-            for i, (other_over, _) in enumerate(across):
-                target = block_of(other_over, 0)
-                found.append((block_of(over, down), 0, target, target == z, i))
+                found.append((block_of(over, down), 1, target, i))
         return found
 
     def relay(block, h, target, i):
@@ -210,16 +246,16 @@
             take_one(block_of(over, down), 0)
         for over, down in along:
             take_one(block_of(over, down), 1)
-        for block, h, target, live, i in relays():
-            @pl.when(jnp.logical_and(live, target != z))
+        for block, h, target, i in relays():
+            @pl.when(target != z)
             def _(block=block, h=h, target=target, i=i):
                 relay(block, h, target, i).start()
         for h, target in late:
             @pl.when(target == z)
             def _(h=h, target=target):
                 one_copy(row, h, target, sent.at[7]).start()
-        for block, h, target, live, i in relays():
-            @pl.when(jnp.logical_and(live, target == z))
+        for block, h, target, i in relays():
+            @pl.when(target == z)
             def _(block=block, h=h, target=target, i=i):
                 relay(block, h, target, i).start()
 
@@ -228,10 +264,6 @@
             take_one(block_of(over, down), 1)
         for over, down in along:
             take_one(block_of(over, down), 0)
-        for block, h, target, live, i in late_relays():
-            @pl.when(live)
-            def _(block=block, h=h, target=target, i=i):
-                relay(block, h, target, i).start()
         for over, down in far:
             take_one(block_of(over, down), 0)
             take_one(block_of(over, down), 1)
@@ -270,6 +302,18 @@
         return remote(second_sent.at[g], second_out.at[half(h), cols(q)], sent.at[9], whole.at[4],
                       device(choose(i, targets), z))
 
+    def via(g):
+        q, i, h = split(g)
+        return remote(second_sent.at[g], passing.at[q, pick(i, [over for over, _ in targets]) - 1], sent.at[9],
+                      pass_recv.at[q, pick(i, [over for over, _ in targets]) - 1],
+                      device(block_of(0, pick(i, [down for _, down in targets])), z))
+
+    def pass_on(q, over):
+        return remote(passing.at[q, over - 1], second_out.at[half(HALVES - 1), cols(q)], sent.at[11], whole.at[4],
+                      device(block_of(over, 0), z))
+
+    middle = jnp.logical_and(a == lax.rem(z, wide), b != lax.div(z, wide))
+
     from_below = jnp.logical_and(z > 0, z <= row)
     from_above = jnp.logical_and(z < rows - 1, z >= row)
 
@@ -308,7 +352,13 @@
         def _():
             chain_down(g).start()
 
-        @pl.when(jnp.logical_and(home, i != rows - 1))
+        turned_off = jnp.logical_and(h == HALVES - 1, i < len(far))
+
+        @pl.when(jnp.logical_and(home, turned_off))
+        def _():
+            via(g).start()
+
+        @pl.when(jnp.logical_and(home, jnp.logical_not(jnp.logical_or(turned_off, i == rows - 1))))
         def _():
             spread(g).start()
 
@@ -458,7 +508,7 @@
     def run(q, order):
         return [q * chunk + sources.index(pair) * HALVES + h for pair in order for h in range(HALVES)]
 
-    table = run(0, [(0, 0)] + across + along + far)
+    table = run(0, sources)
     ends = [chunk - 1]
     for q in range(1, strips):
         if q <= 2:
@@ -477,19 +527,19 @@
             found.append(max(begin, found[-1] + length) if found else begin)
         return found
 
-    kinds = [starts(0, 0, 1), starts(4, 0, (parts + 1) // 2), starts(6, 2, parts), starts(13, 2, parts)]
+    kinds = [starts(0, 0, 1), starts(4, 0, (parts + 1) // 2), starts(6, 2, (parts + 1) // 2), starts(14, 2, 1)]
 
     def by_kind(values):
         return jnp.where(last, values[0], jnp.where(soon, values[1], jnp.where(home, values[3], values[2])))
 
-    per = by_kind([parts, 2, 1, 1])
-    span = by_kind([1, (parts + 1) // 2, parts, parts])
-    home_lag = max(kinds[3][0] + parts, chunk + 1 + 4 * (rows - 1))
-    second_lag = jnp.where(last, chunk - 1, jnp.where(home, home_lag, chunk + 1 + 4 * back))
-    second_slot = by_kind([kind[0] for kind in kinds]) + jnp.where(last, 0, span)
+    per = by_kind([parts, 2, 2, parts])
+    span = by_kind([1, (parts + 1) // 2, (parts + 1) // 2, 1])
+    home_lag = max(kinds[3][0] + 2, chunk + 4 * (rows - 1))
+    second_lag = jnp.where(last, chunk - 1, jnp.where(home, home_lag, chunk + 4 * back))
+    second_slot = by_kind([kind[0] for kind in kinds]) + jnp.where(jnp.logical_or(last, home), 0, span)
     open_slot = by_kind([kind[-1] for kind in kinds]) + 2
     open_limit = max(kind[-1] for kind in kinds) + 1 + opening
-    close_slot = open_limit + by_kind([6, 6, 8, 12])
+    close_slot = open_limit + by_kind([6, 6, 8, 11])
     relay_slot = pick(jnp.abs(z - row), [8, 4, 2] + [1] * rows)
     feed_slot = chunk + 1 - jnp.minimum(jnp.abs(z - row), 4)
     slots = pieces + 1 + home_lag + shift
@@ -505,6 +555,11 @@
             @pl.when(t == feed_slot + (q_ - 2) * (chunk - HALVES))
             def _(q_=q_):
                 feeds(q_)
+
+        for q_ in detours[1:]:
+            @pl.when(jnp.logical_and(helper, t == ends[q_ - 1]))
+            def _(q_=q_):
+                hand_over(q_)
 
         @pl.when(t < pieces)
         def _():
@@ -555,7 +610,11 @@
         def second_count(t):
             ahead = t - second_lag + 1
             count = jnp.maximum(jnp.minimum(ahead, 2 * chunk), ahead - shift)
-            count = jnp.maximum(count, jnp.where(soon, jnp.minimum(ahead + 2, chunk), 0))
+            count = jnp.maximum(count, jnp.where(soon, jnp.minimum(ahead + 1, chunk), 0))
+            burst = 2 * (t - ends[-1] + 1)
+            for end in ends[:-1]:
+                burst = jnp.maximum(burst, 0) + jnp.where(t >= end, chunk, 0)
+            count = jnp.where(last, burst, count)
             return jnp.where(t < second_slot, 0, jnp.clip(count, 0, pieces))
 
         def second(g, _):
@@ -589,6 +648,13 @@
             h, columns = lax.div(turn, tiles), at(lax.rem(turn, tiles) * tile, tile)
             first_own[half(h), columns] = first_tile(row, h, columns)
 
+        for q_ in range(strips):
+            @pl.when(jnp.logical_and(middle, t == home_lag + q_ * chunk + HALVES + shift + 3))
+            def _(q_=q_):
+                for over, _ in across:
+                    arrived(passing.at[q_, over - 1], pass_recv.at[q_, over - 1])
+                    pass_on(q_, over).start()
+
         @pl.when(t == last_slot)
         def _():
             first_last()
@@ -608,6 +674,14 @@
     @pl.when(home)
     def _():
         arrived(second_sent.at[pl.ds(0, pieces - strips * HALVES)], sent.at[9])
+
+    @pl.when(middle)
+    def _():
+        arrived(passing, sent.at[11])
+
+    @pl.when(helper)
+    def _():
+        arrived(handed, sent.at[12])
 
     @pl.when(jnp.logical_and(z >= row, z < rows - 1))
     def _():
@@ -622,10 +696,8 @@
     arrived(weighted.at[other], sent.at[5])
     arrived(pair.at[core], sent.at[6])
     arrived(one.at[core, pl.ds(0, len(across + along))], sent.at[7])
-    for block, h, target, live, i in relays() + late_relays():
-        @pl.when(live)
-        def _(block=block, h=h, target=target, i=i):
-            relay(block, h, target, i).wait_send()
+    for block, h, target, i in relays():
+        relay(block, h, target, i).wait_send()
 
     arrived(first_sent.at[pl.ds(0, rows - 1)], sent.at[10])
 
@@ -705,6 +777,8 @@
             held(wide - 1, part, width),
             held(deep - 1, part, width),
             pltpu.VMEM((samples, width), jnp.float32),
+            held(strips, wide - 1, part, strip),
+            held((strips + 1) // 2, deep - 1, samples, strip),
             dma((4,)),
             dma((pieces,)),
             dma((rows, HALVES, max(wide, deep) - 1)),
@@ -715,7 +789,9 @@
             dma((descent,)),
             dma((wide - 1,)),
             dma((deep - 1,)),
-            dma((11,)),
+            dma((strips, wide - 1)),
+            dma(((strips + 1) // 2, deep - 1, HALVES)),
+            dma((13,)),
             dma((5,)),
         ],
         compiler_params=pltpu.CompilerParams(collective_id=0, has_side_effects=True, vmem_limit_bytes=62 * 2**20),

time: 166 us -> 164 us (0.988)
  Pallas kernels: 165 us -> 163 us
    pallas_call x1, Pallas kernels: 163 us -> 160 us  [per_device(): pl.pallas_call(lambda *refs: step_kernel(rows, strip, *refs), out_shape=(...]
where the time goes in v5:
time: 164 us; the launch traced here: 163 us
  Pallas kernels  163 us (99%)
    pallas_call x1, Pallas kernels, per_device(): pl.pallas_call(lambda *refs: step_kernel(rows, strip, *refs), out_shape=(...  160 us

profile of v5, /device:TPU:0, one launch (start us, length us, event | category | flops | bytes accessed | tf_op | source)
XLA Modules:
  0.0 163.5 jit_solution(11254157210188304436)
XLA Ops:
  0.6 160.4 %twins_step.1 = (bf16[512,1024]{1,0:T(8,128)(2,1)}, bf16[512,1024]{1,0:T(8,128)(2,1)}) custom-call(bf16[512,1024]{1,0:T(8,128)(2,1)} %refs_0_.1, bf16[512,1024]{1,0:T(8,128)(2,1)} %refs_1_.1, bf16[2048,1024]{1,0:T(8,128)(2,1)} %refs_2_.1), custom_call_target="tpu_custom_call" | custom-call | tf_op jit(solution)/shard_map/twins_step/pallas_call | solution.py:756
  161.1 2.4 %settle_grads.1 = (bf16[512,1024]{1,0:T(8,128)(2,1)}, bf16[512,1024]{1,0:T(8,128)(2,1)}) custom-call(bf16[512,1024]{1,0:T(8,128)(2,1)} %get-tuple-element.4.first_ref, bf16[512,1024]{1,0:T(8,128)(2,1)} %get-tuple-element.5.second_ref), custom_call_target="tpu_custom_call" | custom-call | tf_op jit(solution)/shard_map/settle_grads/pallas_call | solution.py:729

commit v6 on v5

--- a/solution.py
+++ b/solution.py
@@ -259,11 +259,13 @@
             def _(block=block, h=h, target=target, i=i):
                 relay(block, h, target, i).start()
 
-    def finish_one():
+    def take_more():
         for over, down in across:
             take_one(block_of(over, down), 1)
         for over, down in along:
             take_one(block_of(over, down), 0)
+
+    def finish_one():
         for over, down in far:
             take_one(block_of(over, down), 0)
             take_one(block_of(over, down), 1)
@@ -527,7 +529,9 @@
             found.append(max(begin, found[-1] + length) if found else begin)
         return found
 
-    kinds = [starts(0, 0, 1), starts(4, 0, (parts + 1) // 2), starts(6, 2, (parts + 1) // 2), starts(14, 2, 1)]
+    kinds = [starts(0, 0, 1), starts(4, 0, (parts + 1) // 2), starts(6, 2, (parts + 1) // 2), [ends[0] + 14]]
+    kinds[3] += [max(ends[min(2, strips - 1)], kinds[3][0]) + q for q in range(1, strips - 1)]
+    kinds[3].append(max(ends[-1], kinds[3][-1] + 1))
 
     def by_kind(values):
         return jnp.where(last, values[0], jnp.where(soon, values[1], jnp.where(home, values[3], values[2])))
@@ -539,7 +543,7 @@
     second_slot = by_kind([kind[0] for kind in kinds]) + jnp.where(jnp.logical_or(last, home), 0, span)
     open_slot = by_kind([kind[-1] for kind in kinds]) + 2
     open_limit = max(kind[-1] for kind in kinds) + 1 + opening
-    close_slot = open_limit + by_kind([6, 6, 8, 11])
+    close_slot = open_limit + by_kind([6, 4, 6, 11])
     relay_slot = pick(jnp.abs(z - row), [8, 4, 2] + [1] * rows)
     feed_slot = chunk + 1 - jnp.minimum(jnp.abs(z - row), 4)
     slots = pieces + 1 + home_lag + shift
@@ -578,6 +582,10 @@
                 @pl.when(t == ends[q_])
                 def _(q_=q_):
                     two_swap(q_).start()
+
+        @pl.when(t == by_kind([chunk - 2, chunk + 1, chunk + 2, kinds[3][0] - 2]))
+        def _():
+            take_more()
 
         @pl.when(t == by_kind([kind[0] for kind in kinds]))
         def _():

time: 164 us -> 163 us (level)
  Pallas kernels: 163 us -> 160 us
    pallas_call x1, Pallas kernels: 160 us -> 158 us  [per_device(): pl.pallas_call(lambda *refs: step_kernel(rows, strip, *refs), out_shape=(...]
where the time goes in v6:
time: 163 us; the launch traced here: 161 us
  Pallas kernels  160 us (98%)
    pallas_call x1, Pallas kernels, per_device(): pl.pallas_call(lambda *refs: step_kernel(rows, strip, *refs), out_shape=(...  158 us

profile of v6, /device:TPU:0, one launch (start us, length us, event | category | flops | bytes accessed | tf_op | source)
XLA Modules:
  0.0 161.1 jit_solution(16388845586664532167)
XLA Ops:
  0.6 158.0 %twins_step.1 = (bf16[512,1024]{1,0:T(8,128)(2,1)}, bf16[512,1024]{1,0:T(8,128)(2,1)}) custom-call(bf16[512,1024]{1,0:T(8,128)(2,1)} %refs_0_.1, bf16[512,1024]{1,0:T(8,128)(2,1)} %refs_1_.1, bf16[2048,1024]{1,0:T(8,128)(2,1)} %refs_2_.1), custom_call_target="tpu_custom_call" | custom-call | tf_op jit(solution)/shard_map/twins_step/pallas_call | solution.py:764
  158.7 2.4 %settle_grads.1 = (bf16[512,1024]{1,0:T(8,128)(2,1)}, bf16[512,1024]{1,0:T(8,128)(2,1)}) custom-call(bf16[512,1024]{1,0:T(8,128)(2,1)} %get-tuple-element.4.first_ref, bf16[512,1024]{1,0:T(8,128)(2,1)} %get-tuple-element.5.second_ref), custom_call_target="tpu_custom_call" | custom-call | tf_op jit(solution)/shard_map/settle_grads/pallas_call | solution.py:737

commit v7 on v6

--- a/solution.py
+++ b/solution.py
@@ -310,6 +310,8 @@
                       pass_recv.at[q, pick(i, [over for over, _ in targets]) - 1],
                       device(block_of(0, pick(i, [down for _, down in targets])), z))
 
+    passes = passing.shape[0]
+
     def pass_on(q, over):
         return remote(passing.at[q, over - 1], second_out.at[half(HALVES - 1), cols(q)], sent.at[11], whole.at[4],
                       device(block_of(over, 0), z))
@@ -354,7 +356,7 @@
         def _():
             chain_down(g).start()
 
-        turned_off = jnp.logical_and(h == HALVES - 1, i < len(far))
+        turned_off = jnp.logical_and(jnp.logical_and(h == HALVES - 1, i < len(far)), q < passes)
 
         @pl.when(jnp.logical_and(home, turned_off))
         def _():
@@ -543,7 +545,7 @@
     second_slot = by_kind([kind[0] for kind in kinds]) + jnp.where(jnp.logical_or(last, home), 0, span)
     open_slot = by_kind([kind[-1] for kind in kinds]) + 2
     open_limit = max(kind[-1] for kind in kinds) + 1 + opening
-    close_slot = open_limit + by_kind([6, 4, 6, 11])
+    close_slot = open_limit + by_kind([6, 4, 6, 9])
     relay_slot = pick(jnp.abs(z - row), [8, 4, 2] + [1] * rows)
     feed_slot = chunk + 1 - jnp.minimum(jnp.abs(z - row), 4)
     slots = pieces + 1 + home_lag + shift
@@ -656,7 +658,7 @@
             h, columns = lax.div(turn, tiles), at(lax.rem(turn, tiles) * tile, tile)
             first_own[half(h), columns] = first_tile(row, h, columns)
 
-        for q_ in range(strips):
+        for q_ in range(passes):
             @pl.when(jnp.logical_and(middle, t == home_lag + q_ * chunk + HALVES + shift + 3))
             def _(q_=q_):
                 for over, _ in across:
@@ -752,6 +754,7 @@
     wide, deep = PAIR, rows // PAIR
     part = samples // HALVES
     pieces = strips * rows * HALVES
+    passes = max(1, strips - 1)
     own = jax.ShapeDtypeStruct((samples, width), jnp.bfloat16)
     any_space = pl.BlockSpec(memory_space=pl.ANY)
     dma = pltpu.SemaphoreType.DMA
@@ -785,7 +788,7 @@
             held(wide - 1, part, width),
             held(deep - 1, part, width),
             pltpu.VMEM((samples, width), jnp.float32),
-            held(strips, wide - 1, part, strip),
+            held(passes, wide - 1, part, strip),
             held((strips + 1) // 2, deep - 1, samples, strip),
             dma((4,)),
             dma((pieces,)),
@@ -797,7 +800,7 @@
             dma((descent,)),
             dma((wide - 1,)),
             dma((deep - 1,)),
-            dma((strips, wide - 1)),
+            dma((passes, wide - 1)),
             dma(((strips + 1) // 2, deep - 1, HALVES)),
             dma((13,)),
             dma((5,)),

time: 163 us -> 161 us (0.988); the launches traced: 161 us -> 161 us
  no operation moved by 1% of the time
where the time goes in v7:
time: 161 us
  Pallas kernels  160 us (99%)
    pallas_call x1, Pallas kernels, per_device(): pl.pallas_call(lambda *refs: step_kernel(rows, strip, *refs), out_shape=(...  158 us

profile of v7, /device:TPU:0, one launch (start us, length us, event | category | flops | bytes accessed | tf_op | source)
XLA Modules:
  0.0 160.9 jit_solution(13712909205609196528)
XLA Ops:
  0.6 157.9 %twins_step.1 = (bf16[512,1024]{1,0:T(8,128)(2,1)}, bf16[512,1024]{1,0:T(8,128)(2,1)}) custom-call(bf16[512,1024]{1,0:T(8,128)(2,1)} %refs_0_.1, bf16[512,1024]{1,0:T(8,128)(2,1)} %refs_1_.1, bf16[2048,1024]{1,0:T(8,128)(2,1)} %refs_2_.1), custom_call_target="tpu_custom_call" | custom-call | tf_op jit(solution)/shard_map/twins_step/pallas_call | solution.py:767
  158.5 2.4 %settle_grads.1 = (bf16[512,1024]{1,0:T(8,128)(2,1)}, bf16[512,1024]{1,0:T(8,128)(2,1)}) custom-call(bf16[512,1024]{1,0:T(8,128)(2,1)} %get-tuple-element.4.first_ref, bf16[512,1024]{1,0:T(8,128)(2,1)} %get-tuple-element.5.second_ref), custom_call_target="tpu_custom_call" | custom-call | tf_op jit(solution)/shard_map/settle_grads/pallas_call | solution.py:739
